TPU v7x, 8 devices: a whole 2x2x1 slice. The times are simulated.
8 devices in a mesh: dp: 2 (over z, y), tp: 4 (over x, core).
Axes of the slice: x: 2, y: 2, z: 1, core: 2. Of those that a mesh axis runs over, the one named last changes fastest.
Arguments:
- hidden: bfloat16 [32, 1024], P('dp'), parts along dimension 0
- lengths: int32 [32], P('dp'), parts along dimension 0
- choice: int32 [2, 32, 8], P(None, 'dp'), parts along dimension 1
- keys_one: bfloat16 [32, 64, 8, 64], P('dp', 'tp'), parts along dimension 0
- vals_one: bfloat16 [32, 64, 8, 64], P('dp', 'tp'), parts along dimension 0
- keys_two: bfloat16 [32, 64, 8, 64], P('dp', 'tp'), parts along dimension 0
- vals_two: bfloat16 [32, 64, 8, 64], P('dp', 'tp'), parts along dimension 0
- g_attn: bfloat16 [2, 1024], replicated
- w_q: bfloat16 [2, 1024, 1024], P(None, None, 'tp')
- w_k: bfloat16 [2, 1024, 512], P(None, None, 'tp')
- w_v: bfloat16 [2, 1024, 512], P(None, None, 'tp')
- w_o: bfloat16 [2, 1024, 1024], P(None, 'tp')
- g_mlp: bfloat16 [2, 1024], replicated
- w_router: bfloat16 [2, 1024, 32], replicated
- w_gate: bfloat16 [2, 32, 1024, 512], P(None, None, None, 'tp')
- w_up: bfloat16 [2, 32, 1024, 512], P(None, None, None, 'tp')
- w_down: bfloat16 [2, 32, 512, 1024], P(None, None, 'tp')
Outputs:
- output 1: bfloat16 [32, 1024], P('dp'), parts along dimension 0
- output 2: bfloat16 [32, 64, 8, 64], P('dp', None, 'tp'), parts along dimension 0
- output 3: bfloat16 [32, 64, 8, 64], P('dp', None, 'tp'), parts along dimension 0
- output 4: bfloat16 [32, 64, 8, 64], P('dp', None, 'tp'), parts along dimension 0
- output 5: bfloat16 [32, 64, 8, 64], P('dp', None, 'tp'), parts along dimension 0
There are 2 independent parts. A program takes and returns all parts, laid end to end along the dimension named above; an argument that names none is the same for every part.
All inputs are finite; a program needn't handle non-finite values.
Results may differ from a plain program's by a relative error of at most 0.02.
Values are sent between devices in bfloat16 or wider.
A program may use at most 1 GiB of HBM per device.

v0:
```python
import jax
import jax.numpy as jnp
from jax import lax
from jax.sharding import PartitionSpec as P

EPS = 1e-5
THETA = 1000000.0


def rms_norm(tensor, gain_vec):
    tensor_f = tensor.astype(jnp.float32)
    scale = lax.rsqrt(jnp.mean(tensor_f * tensor_f, axis=-1, keepdims=True) + EPS)
    return (tensor_f * scale * gain_vec.astype(jnp.float32)).astype(jnp.bfloat16)


def apply_rope(tensor, lengths):
    head_dim = tensor.shape[-1]
    half_dim = head_dim // 2
    inv_freq = THETA ** (-2.0 * jnp.arange(half_dim, dtype=jnp.float32) / head_dim)
    angle = lengths.astype(jnp.float32)[:, None] * inv_freq[None, :]
    cos_part = jnp.cos(angle)[:, None, :]
    sin_part = jnp.sin(angle)[:, None, :]
    lower_half = tensor[..., :half_dim]
    upper_half = tensor[..., half_dim:]
    return jnp.concatenate([lower_half * cos_part - upper_half * sin_part, upper_half * cos_part + lower_half * sin_part], axis=-1)


def expert_block(x_mid, choice, g_mlp, w_router, w_gate, w_up, w_down):
    normed = rms_norm(x_mid, g_mlp)
    logits = jnp.dot(normed, w_router, preferred_element_type=jnp.float32)
    onehot = (choice[:, :, None] == jnp.arange(w_router.shape[1])[None, None, :]).astype(jnp.float32)
    gate_prob = jax.nn.softmax(jnp.sum(onehot * logits[:, None, :], axis=-1), axis=-1)
    gate_mat = jnp.sum(gate_prob[:, :, None] * onehot, axis=1)
    gate_act = jnp.einsum('bd,edf->bef', normed, w_gate, preferred_element_type=jnp.float32)
    up_act = jnp.einsum('bd,edf->bef', normed, w_up, preferred_element_type=jnp.float32)
    expert_in = (jax.nn.silu(gate_act) * up_act * gate_mat[:, :, None]).astype(jnp.bfloat16)
    return jnp.einsum('bef,efd->bd', expert_in, w_down, preferred_element_type=jnp.float32)


def decode_layer(hidden, lengths, choice, key_cache, val_cache, g_attn, w_q, w_k, w_v, w_o, g_mlp, w_router, w_gate, w_up, w_down):
    batch_rows, seq_len, kv_heads, head_dim = key_cache.shape
    num_heads = w_q.shape[1] // head_dim
    normed = rms_norm(hidden, g_attn)
    query_rot = apply_rope(jnp.dot(normed, w_q, preferred_element_type=jnp.float32).reshape(batch_rows, num_heads, head_dim), lengths).astype(jnp.bfloat16)
    key_new = apply_rope(jnp.dot(normed, w_k, preferred_element_type=jnp.float32).reshape(batch_rows, kv_heads, head_dim), lengths).astype(jnp.bfloat16)
    val_new = jnp.dot(normed, w_v, preferred_element_type=jnp.float32).astype(jnp.bfloat16).reshape(batch_rows, kv_heads, head_dim)
    positions = jnp.arange(seq_len)
    is_new = (positions[None, :] == lengths[:, None])[:, :, None, None]
    key_cache = jnp.where(is_new, key_new[:, None], key_cache)
    val_cache = jnp.where(is_new, val_new[:, None], val_cache)
    query_grp = query_rot.reshape(batch_rows, kv_heads, num_heads // kv_heads, head_dim)
    scores = jnp.einsum('bgrd,bsgd->bgrs', query_grp, key_cache, preferred_element_type=jnp.float32) * head_dim ** -0.5
    is_valid = (positions[None, :] <= lengths[:, None])[:, None, None, :]
    attn_prob = jax.nn.softmax(jnp.where(is_valid, scores, -1e30), axis=-1).astype(jnp.bfloat16)
    attn_vec = jnp.einsum('bgrs,bsgd->bgrd', attn_prob, val_cache, preferred_element_type=jnp.float32).astype(jnp.bfloat16).reshape(batch_rows, num_heads * head_dim)
    attn_sum = lax.psum(jnp.dot(attn_vec, w_o, preferred_element_type=jnp.float32).astype(jnp.bfloat16), 'tp')
    x_mid = (hidden.astype(jnp.float32) + attn_sum.astype(jnp.float32)).astype(jnp.bfloat16)
    moe_sum = lax.psum(expert_block(x_mid, choice, g_mlp, w_router, w_gate, w_up, w_down).astype(jnp.bfloat16), 'tp')
    return (x_mid.astype(jnp.float32) + moe_sum.astype(jnp.float32)).astype(jnp.bfloat16), key_cache, val_cache


def solution(mesh):
    seq_spec = P('dp', 'tp', None, None)
    head_spec = P('dp', None, 'tp', None)
    col_spec = P(None, None, 'tp')
    ff_spec = P(None, None, None, 'tp')

    def local_step(hidden, lengths, choice, keys_one, vals_one, keys_two, vals_two, g_attn, w_q, w_k, w_v, w_o, g_mlp, w_router, w_gate, w_up, w_down):
        moved = [lax.all_to_all(cache_blk, 'tp', 2, 1, tiled=True) for cache_blk in (keys_one, vals_one, keys_two, vals_two)]
        results = []
        for layer_idx in range(2):
            hidden, key_cache, val_cache = decode_layer(hidden, lengths, choice[layer_idx], moved[2 * layer_idx], moved[2 * layer_idx + 1], g_attn[layer_idx], w_q[layer_idx], w_k[layer_idx], w_v[layer_idx], w_o[layer_idx], g_mlp[layer_idx], w_router[layer_idx], w_gate[layer_idx], w_up[layer_idx], w_down[layer_idx])
            results.append(key_cache)
            results.append(val_cache)
        return (hidden, results[0], results[1], results[2], results[3])

    return jax.shard_map(local_step, mesh=mesh, in_specs=(P('dp', None), P('dp'), P(None, 'dp', None), seq_spec, seq_spec, seq_spec, seq_spec, P(), col_spec, col_spec, col_spec, P(None, 'tp', None), P(), P(), ff_spec, ff_spec, P(None, None, 'tp', None)), out_specs=(P('dp', None), head_spec, head_spec, head_spec, head_spec), check_vma=False)
```

profile of v0, /device:TPU:0, one launch (start us, length us, event | category | flops | bytes accessed | tf_op | source)
XLA Modules:
  0.0 129.6 jit_solution(13590160122453047711)
XLA Ops:
  0.7 1.2 copy.115
  1.9 1.1 reshape.280
  3.0 4.6 %all-to-all-start = ((bf16[4,2,16384]{2,1,0:T(2,128)(2,1)}), bf16[4,2,16384]{2,1,0:T(2,128)(2,1)S(1)}, u32[]{:S(2)}, u32[]{:S(2)}) async-start(bf16[4,2,16384]{2,1,0:T(2,128)(2,1)} %reshape.280), calls=%async_computation | async-start | bytes 524288 | tf_op jit(solution)/shard_map/all_to_all | solution.py:69
  9.2 1.1 slice_bitcast_fusion.2
  12.4 1.2 convolution_convert_fusion.5
  13.7 1.1 copy.114
  14.8 1.1 reshape.278
  15.9 1.3 slice_bitcast_fusion
  17.4 1.1 fusion.120
  20.4 1.1 copy.113
  21.5 1.1 reshape.282
  22.6 1.1 copy.112
  23.7 1.1 reshape.276
  25.6 3.4 %all-to-all-start.1 = ((bf16[4,2,16384]{2,1,0:T(2,128)(2,1)}), bf16[4,2,16384]{2,1,0:T(2,128)(2,1)S(1)}, u32[]{:S(2)}, u32[]{:S(2)}) async-start(bf16[4,2,16384]{2,1,0:T(2,128)(2,1)} %reshape.278), calls=%async_computation.1 | async-start | bytes 524288 | tf_op jit(solution)/shard_map/all_to_all | solution.py:69
  29.1 1.3 %iota_compare_fusion.3 = (pred[16,64]{1,0:T(8,128)(4,1)}, pred[16,64]{1,0:T(8,128)(4,1)S(1)}) fusion(s32[16]{0:T(128)} %param.18), kind=kLoop, calls=%fused_computation.155 | loop fusion | flops 2048 | bytes 2112 | tf_op jit(solution)/shard_map/le | solution.py:53
  31.3 3.6 %all-to-all-done.1 = bf16[4,2,16384]{2,1,0:T(2,128)(2,1)S(1)} async-done(((bf16[4,2,16384]{2,1,0:T(2,128)(2,1)}), bf16[4,2,16384]{2,1,0:T(2,128)(2,1)S(1)}, u32[]{:S(2)}, u32[]{:S(2)}) %all-to-all-start.1) | async-done | bytes 262176 | tf_op jit(solution)/shard_map/all_to_all | solution.py:69
  34.8 3.4 %all-to-all-start.2 = ((bf16[4,2,16384]{2,1,0:T(2,128)(2,1)}), bf16[4,2,16384]{2,1,0:T(2,128)(2,1)S(1)}, u32[]{:S(2)}, u32[]{:S(2)}) async-start(bf16[4,2,16384]{2,1,0:T(2,128)(2,1)} %reshape.282), calls=%async_computation.2 | async-start | bytes 524288 | tf_op jit(solution)/shard_map/all_to_all | solution.py:69
  39.2 2.4 %broadcast_select_fusion.3 = (bf16[16,64,2,64]{3,2,1,0:T(2,128)(2,1)S(1)}, bf16[16,64,2,64]{3,2,1,0:T(2,128)(2,1)}) fusion(bf16[16,64,2,64]{3,2,1,0:T(2,128)(2,1)S(1)} %bitcast.166, pred[16,64]{1,0:T(8,128)(4,1)S(1)} %get-tuple-element.32, bf16[16,2,64]{2,1,0:T(2,128)(2,1)S(1)} %copy.70, bf16[16,64,2,64]{3,2,1,0:T(2,128)(2,1)S(1)} %bitcast.169, ...), kind=kLoop, calls=%fused_computation.47 | loop fusion | flops 262144 | bytes 1057792 | tf_op jit(solution)/shard_map/jit(_where)/select_n | solution.py:49
  41.6 1.1 fusion.54
  43.0 1.6 %convolution_convert_fusion.3 = bf16[16,2,2,64]{3,2,1,0:T(2,128)(2,1)S(1)} fusion(bf16[16,64,2,64]{3,2,1,0:T(2,128)(2,1)} %get-tuple-element.28, f32[16,2,2]{2,1,0:T(2,128)S(1)} %fusion.145, f32[16,2,2,64]{3,2,1,0:T(2,128)S(1)} %fusion.54), kind=kOutput, calls=%fused_computation.41 | convolution fusion | flops 540799 | bytes 286976 | tf_op jit(solution)/shard_map/bgrs,bsgd->bgrd/dot_general | solution.py:55
  44.8 11.9 %psum.28 = bf16[16,1024]{1,0:T(8,128)(2,1)S(1)} all-reduce(bf16[16,1024]{1,0:T(8,128)(2,1)S(1)} %convolution_convert_fusion.1), channel_id=1, replica_groups=mesh['dp'=2,'tp'=4] {'tp'}, use_global_device_ids=true, to_apply=%region_3.4 | all-reduce | flops 16384 | bytes 65536 | tf_op jit(solution)/shard_map/psum | solution.py:56
  58.6 4.6 %fusion.12 = f32[16,32,128]{2,0,1:T(8,128)S(1)} fusion(bf16[2,32,1024,128]{3,2,1,0:T(8,128)(2,1)} %param.31, bf16[16,1024]{1,0:T(8,128)(2,1)S(1)} %fusion.92), kind=kOutput, calls=%fused_computation.12 | convolution fusion | flops 134217728 | bytes 8683520 | tf_op jit(solution)/shard_map/bd,edf->bef/dot_general | solution.py:34
  63.2 7.1 %fusion.47 = bf16[16,1024]{1,0:T(8,128)(2,1)S(1)} fusion(bf16[2,32,128,1024]{3,2,1,0:T(8,128)(2,1)} %param.33, bf16[2,32,1024,128]{3,2,1,0:T(8,128)(2,1)} %param.32, f32[16,32,128]{2,0,1:T(8,128)S(1)} %fusion.12, f32[16,32]{0,1:T(8,128)S(1)} %copy.80, bf16[16,1024]{1,0:T(8,128)(2,1)S(1)} %fusion.92), kind=kOutput, calls=%fused_computation.29 | convolution fusion | flops 268910592 | bytes 17106944 | tf_op jit(solution)/shard_map/bef,efd->bd/dot_general | solution.py:37
  70.3 10.3 %psum.29 = bf16[16,1024]{1,0:T(8,128)(2,1)S(1)} all-reduce(bf16[16,1024]{1,0:T(8,128)(2,1)S(1)} %fusion.47), channel_id=1, replica_groups=mesh['dp'=2,'tp'=4] {'tp'}, use_global_device_ids=true, to_apply=%region_9.10 | all-reduce | flops 16384 | bytes 65536 | tf_op jit(solution)/shard_map/psum | solution.py:58
  80.7 1.2 convolution_convert_fusion.4
  82.6 3.6 %all-to-all-start.3 = ((bf16[4,2,16384]{2,1,0:T(2,128)(2,1)}), bf16[4,2,16384]{2,1,0:T(2,128)(2,1)S(1)}, u32[]{:S(2)}, u32[]{:S(2)}) async-start(bf16[4,2,16384]{2,1,0:T(2,128)(2,1)} %reshape.276), calls=%async_computation.3 | async-start | bytes 524288 | tf_op jit(solution)/shard_map/all_to_all | solution.py:69
  87.4 4.4 %all-to-all-done.3 = bf16[4,2,16384]{2,1,0:T(2,128)(2,1)S(1)} async-done(((bf16[4,2,16384]{2,1,0:T(2,128)(2,1)}), bf16[4,2,16384]{2,1,0:T(2,128)(2,1)S(1)}, u32[]{:S(2)}, u32[]{:S(2)}) %all-to-all-start.3) | async-done | bytes 262176 | tf_op jit(solution)/shard_map/all_to_all | solution.py:69
  92.7 1.5 %broadcast_select_fusion.1 = (bf16[16,64,2,64]{3,2,1,0:T(2,128)(2,1)S(1)}, bf16[16,64,2,64]{3,2,1,0:T(2,128)(2,1)S(1)}) fusion(bf16[16,64,2,64]{3,2,1,0:T(2,128)(2,1)S(1)} %bitcast.167, pred[16,64]{1,0:T(8,128)(4,1)S(1)} %get-tuple-element.32, bf16[16,2,64]{2,1,0:T(2,128)(2,1)S(1)} %copy.85, bf16[16,64,2,64]{3,2,1,0:T(2,128)(2,1)S(1)} %bitcast.168, ...), kind=kLoop, calls=%fused_computation.45 | loop fusion | flops 262144 | bytes 1057792 | tf_op jit(solution)/shard_map/jit(_where)/select_n | solution.py:49
  95.7 10.3 %psum.30 = bf16[16,1024]{1,0:T(8,128)(2,1)S(1)} all-reduce(bf16[16,1024]{1,0:T(8,128)(2,1)S(1)} %convolution_convert_fusion), channel_id=1, replica_groups=mesh['dp'=2,'tp'=4] {'tp'}, use_global_device_ids=true, to_apply=%region_13.14 | all-reduce | flops 16384 | bytes 65536 | tf_op jit(solution)/shard_map/psum | solution.py:56
  106.3 4.6 %fusion.6 = f32[16,32,128]{2,0,1:T(8,128)S(1)} fusion(bf16[2,32,1024,128]{3,2,1,0:T(8,128)(2,1)} %param.31, bf16[16,1024]{1,0:T(8,128)(2,1)S(1)} %fusion.100), kind=kOutput, calls=%fused_computation.6 | convolution fusion | flops 134217728 | bytes 8683520 | tf_op jit(solution)/shard_map/bd,edf->bef/dot_general | solution.py:34
  111.6 7.1 %fusion.44 = bf16[16,1024]{1,0:T(8,128)(2,1)S(1)} fusion(bf16[2,32,128,1024]{3,2,1,0:T(8,128)(2,1)} %param.33, bf16[2,32,1024,128]{3,2,1,0:T(8,128)(2,1)} %param.32, f32[16,32,128]{2,0,1:T(8,128)S(1)} %fusion.6, f32[16,32]{0,1:T(8,128)S(1)} %copy.95, bf16[16,1024]{1,0:T(8,128)(2,1)S(1)} %fusion.100), kind=kOutput, calls=%fused_computation.28 | convolution fusion | flops 268910592 | bytes 17106944 | tf_op jit(solution)/shard_map/bef,efd->bd/dot_general | solution.py:37
  118.7 10.3 %psum.31 = bf16[16,1024]{1,0:T(8,128)(2,1)S(1)} all-reduce(bf16[16,1024]{1,0:T(8,128)(2,1)S(1)} %fusion.44), channel_id=1, replica_groups=mesh['dp'=2,'tp'=4] {'tp'}, use_global_device_ids=true, to_apply=%region_19.20 | all-reduce | flops 16384 | bytes 65536 | tf_op jit(solution)/shard_map/psum | solution.py:58
  (86 shorter events, 17.0 us)
Async XLA Ops:
  0.6 56.0 %copy-start = (bf16[16,1024]{1,0:T(8,128)(2,1)S(1)}, bf16[16,1024]{1,0:T(8,128)(2,1)}, u32[]{:S(2)}) copy-start(bf16[16,1024]{1,0:T(8,128)(2,1)} %param.17) | copy-start | bytes 98308
  0.6 44.0 %copy-start.1 = (bf16[2,256,1024]{2,1,0:T(8,128)(2,1)S(1)}, bf16[2,256,1024]{2,1,0:T(8,128)(2,1)}, u32[]{:S(2)}) copy-start(bf16[2,256,1024]{2,1,0:T(8,128)(2,1)} %param.28) | copy-start | bytes 3145732
  3.0 22.7 %all-to-all-start = ((bf16[4,2,16384]{2,1,0:T(2,128)(2,1)}), bf16[4,2,16384]{2,1,0:T(2,128)(2,1)S(1)}, u32[]{:S(2)}, u32[]{:S(2)}) async-start(bf16[4,2,16384]{2,1,0:T(2,128)(2,1)} %reshape.280), calls=%async_computation | async-start | bytes 524288 | tf_op jit(solution)/shard_map/all_to_all | solution.py:69
  25.6 9.2 %all-to-all-start.1 = ((bf16[4,2,16384]{2,1,0:T(2,128)(2,1)}), bf16[4,2,16384]{2,1,0:T(2,128)(2,1)S(1)}, u32[]{:S(2)}, u32[]{:S(2)}) async-start(bf16[4,2,16384]{2,1,0:T(2,128)(2,1)} %reshape.278), calls=%async_computation.1 | async-start | bytes 524288 | tf_op jit(solution)/shard_map/all_to_all | solution.py:69
  34.8 47.7 %all-to-all-start.2 = ((bf16[4,2,16384]{2,1,0:T(2,128)(2,1)}), bf16[4,2,16384]{2,1,0:T(2,128)(2,1)S(1)}, u32[]{:S(2)}, u32[]{:S(2)}) async-start(bf16[4,2,16384]{2,1,0:T(2,128)(2,1)} %reshape.282), calls=%async_computation.2 | async-start | bytes 524288 | tf_op jit(solution)/shard_map/all_to_all | solution.py:69
  41.6 45.8 %copy-start.2 = (bf16[16,64,2,64]{3,2,1,0:T(2,128)(2,1)}, bf16[16,64,2,64]{3,2,1,0:T(2,128)(2,1)S(1)}, u32[]{:S(2)}) copy-start(bf16[16,64,2,64]{3,2,1,0:T(2,128)(2,1)S(1)} %get-tuple-element.27) | copy-start | bytes 786436
  58.6 35.6 %copy-start.6 = (pred[16,64]{1,0:T(8,128)(4,1)S(1)}, pred[16,64]{1,0:T(8,128)(4,1)}, u32[]{:S(2)}) copy-start(pred[16,64]{1,0:T(8,128)(4,1)} %get-tuple-element.31) | copy-start | bytes 3076
  63.2 42.9 %copy-start.5 = (bf16[2,1024,32]{1,2,0:T(8,128)(2,1)S(1)}, bf16[2,1024,32]{1,2,0:T(8,128)(2,1)}, u32[]{:S(2)}) copy-start(bf16[2,1024,32]{1,2,0:T(8,128)(2,1)} %param.30) | copy-start | bytes 393220
  82.6 9.2 %all-to-all-start.3 = ((bf16[4,2,16384]{2,1,0:T(2,128)(2,1)}), bf16[4,2,16384]{2,1,0:T(2,128)(2,1)S(1)}, u32[]{:S(2)}, u32[]{:S(2)}) async-start(bf16[4,2,16384]{2,1,0:T(2,128)(2,1)} %reshape.276), calls=%async_computation.3 | async-start | bytes 524288 | tf_op jit(solution)/shard_map/all_to_all | solution.py:69
  94.2 35.4 %copy-start.3 = (bf16[16,64,2,64]{3,2,1,0:T(2,128)(2,1)}, bf16[16,64,2,64]{3,2,1,0:T(2,128)(2,1)S(1)}, u32[]{:S(2)}) copy-start(bf16[16,64,2,64]{3,2,1,0:T(2,128)(2,1)S(1)} %get-tuple-element.25) | copy-start | bytes 786436
  94.2 35.4 %copy-start.4 = (bf16[16,64,2,64]{3,2,1,0:T(2,128)(2,1)}, bf16[16,64,2,64]{3,2,1,0:T(2,128)(2,1)S(1)}, u32[]{:S(2)}) copy-start(bf16[16,64,2,64]{3,2,1,0:T(2,128)(2,1)S(1)} %get-tuple-element.26) | copy-start | bytes 786436
where the time goes:
time: 131 us; the launch traced here: 130 us
  blocking collectives  42.7 us (33%)
  matrix products  33.4 us (25%)
  local copies, waits for them, and re-layouts  17.6 us (13%)
  starting transfers between devices  15 us (11%)
  other arithmetic  12 us (9%)
  waiting for transfers between devices  7.97 us (6%)
    psum x2, blocking collectives, decode_layer(): lax.psum(jnp.dot(attn_vec, w_o, preferred_element_type=jnp.float32).astyp...  22.1 us
    psum x2, blocking collectives, decode_layer(): lax.psum(expert_block(x_mid, choice, g_mlp, w_router, w_gate, w_up, w_dow...  20.5 us
    all_to_all x4, starting transfers between devices, local_step(): lax.all_to_all(cache_blk, 'tp', 2, 1, tiled=True)  15 us
    dot_general x2, matrix products, expert_block(): jnp.einsum('bef,efd->bd', expert_in, w_down, preferred_element_type=jnp.f...  14.2 us
    unnamed x26, local copies, waits for them, and re-layouts  10.3 us
    dot_general x2, matrix products, expert_block(): jnp.einsum('bd,edf->bef', normed, w_gate, preferred_element_type=jnp.floa...  9.17 us
    all_to_all x4, waiting for transfers between devices, local_step(): lax.all_to_all(cache_blk, 'tp', 2, 1, tiled=True)  7.97 us
    select_n x2, other arithmetic, decode_layer(): key_cache = jnp.where(is_new, key_new[:, None], key_cache)  3.9 us
  transfers between devices with their start and end apart: 4, of which 2 were waited for; matrix products, arithmetic and copies ran while one was open for 33% of the time, Pallas kernels for 0%

commit v1 on v0

v1 whole, which is shorter than its diff:
```python
import functools

import numpy as np

import jax
import jax.numpy as jnp
from jax import lax
from jax.experimental import pallas as pl
from jax.experimental.pallas import tpu as pltpu
from jax.sharding import PartitionSpec as P

EPS = 1e-5
THETA = 1000000.0
MESH = pl.DeviceIdType.MESH
B = 16
D = 1024
SEQ = 64
BLK = 16
NTP = 4
EXP = 32
FL = 128
GCH = 4
DCH = 8
NCH = 512
F32 = jnp.float32
BF16 = jnp.bfloat16


def _norm(h_f, gain_row):
    scale = lax.rsqrt(jnp.mean(h_f * h_f, axis=-1, keepdims=True) + EPS)
    return (h_f * scale * gain_row).astype(BF16)


def _rope(x, cosv, sinv, low):
    rot = jnp.where(low, -pltpu.roll(x, 96, 1), pltpu.roll(x, 32, 1))
    return x * cosv + rot * sinv


def _kernel(hid_h, len_h, cho_h, k1_h, v1_h, k2_h, v2_h, ga_h, wq_h, wk_h, wv_h, wo_h, gm_h, wr_h, wg_h, wu_h, wd_h, inv_h,
            hout_h, ok1_h, ov1_h, ok2_h, ov2_h,
            hid, lens, cho, raw, ga, wq, wk, wv, wo, gm, wr, wg, wu, wd, inv,
            spread, snd, kall, xown, xrecv, gexp, act, hfin,
            sem_s, sem_raw, sem_g, sem_u, sem_d, send_c, recv_c, send_x, recv_x, sem_o):
    me = lax.axis_index("tp")
    chip, core = me // 2, me % 2
    partner = chip * 2 + (1 - core)
    cross_a = (1 - chip) * 2 + core
    cross_b = (1 - chip) * 2 + (1 - core)
    peers = (cross_a, cross_b, partner)

    barrier = pltpu.get_barrier_semaphore()
    for p in peers:
        pl.semaphore_signal(barrier, inc=1, device_id={"tp": p}, device_id_type=MESH)

    raw_src = (k1_h, v1_h, k2_h, v2_h)

    def raw_copy(c):
        return pltpu.make_async_copy(raw_src[c], raw.at[c], sem_raw.at[c])

    smalls = ((hid_h, hid), (len_h, lens), (cho_h, cho), (ga_h, ga), (gm_h, gm), (inv_h, inv),
              (wq_h, wq), (wk_h, wk), (wv_h, wv), (wo_h, wo), (wr_h, wr))

    def small_copy(i):
        return pltpu.make_async_copy(smalls[i][0], smalls[i][1], sem_s.at[i])

    def g_copy(l, i):
        sl = pl.ds(i * GCH, GCH)
        return pltpu.make_async_copy(wg_h.at[l, sl], wg.at[l, sl], sem_g.at[l, i])

    def u_copy(l, i):
        sl = pl.ds(i * GCH, GCH)
        return pltpu.make_async_copy(wu_h.at[l, sl], wu.at[l, sl], sem_u.at[l, i])

    def d_copy(l, i):
        sl = pl.ds(i * DCH, DCH)
        return pltpu.make_async_copy(wd_h.at[l, sl], wd.at[l, sl], sem_d.at[l, i])

    raw_copy(0).start()
    raw_copy(1).start()
    for i in range(len(smalls)):
        small_copy(i).start()
    raw_copy(2).start()
    raw_copy(3).start()

    def start_layer(l):
        def gu(i, _):
            g_copy(l, i).start()
            u_copy(l, i).start()
            return 0
        lax.fori_loop(0, EXP // GCH, gu, 0)

        def dn(i, _):
            d_copy(l, i).start()
            return 0
        lax.fori_loop(0, EXP // DCH, dn, 0)

    def cache_copy(c, n):
        return pltpu.make_async_remote_copy(
            src_ref=snd.at[c, peers[n]], dst_ref=kall.at[c, me],
            send_sem=send_c.at[c, n], recv_sem=recv_c.at[c, me],
            device_id={"tp": peers[n]}, device_id_type=MESH)

    def cache_recv(c, n):
        return pltpu.make_async_remote_copy(
            src_ref=snd.at[c, peers[n]], dst_ref=kall.at[c, peers[n]],
            send_sem=send_c.at[c, n], recv_sem=recv_c.at[c, peers[n]],
            device_id={"tp": peers[n]}, device_id_type=MESH)

    def repack(c):
        raw_copy(c).wait()
        spread[...] = raw[c].reshape(B * BLK * 8, 64).astype(F32)
        for p in range(NTP):
            lo = spread[pl.ds(2 * p, B * BLK, stride=8), :]
            hi = spread[pl.ds(2 * p + 1, B * BLK, stride=8), :]
            snd[c, p] = jnp.concatenate([lo, hi], axis=1).astype(BF16).reshape(B, BLK, 128)
        kall[c, me] = snd[c, me]

    repack(0)
    pl.semaphore_wait(barrier, 3)
    for n in range(3):
        cache_copy(0, n).start()
    repack(1)
    for n in range(3):
        cache_copy(1, n).start()
    start_layer(0)
    start_layer(1)
    repack(2)
    repack(3)
    for c in (2, 3):
        cache_copy(c, 2).start()

    for i in range(len(smalls)):
        small_copy(i).wait()

    eye = lax.broadcasted_iota(jnp.int32, (B, B), 0) == lax.broadcasted_iota(jnp.int32, (B, B), 1)
    len_row = jnp.broadcast_to(lens[...].astype(F32), (B, B))
    len_col = jnp.sum(jnp.where(eye, len_row, 0.0), axis=1, keepdims=True)
    len_b = jnp.broadcast_to(len_col, (B, 128))
    angle = len_b * inv[...]
    cosv, sinv = jnp.cos(angle), jnp.sin(angle)
    lane = lax.broadcasted_iota(jnp.int32, (B, 128), 1)
    low = (lane % 64) < 32
    left = lane < 64
    col = lax.broadcasted_iota(jnp.int32, (64, 1024), 1)
    row = lax.broadcasted_iota(jnp.int32, (64, 1024), 0)
    len64 = jnp.concatenate([len_col] * 4, axis=0)
    pos = ((col // 256) * BLK + col % BLK).astype(F32)
    valid = (((col // BLK) % B) == (row % B)) & (pos <= len64)

    h_f = hid[...].astype(F32)

    def insert(c, new):
        new3 = jnp.broadcast_to(new[:, None, :], (B, BLK, 128))
        len3 = jnp.broadcast_to(len_b[:, None, :], (B, BLK, 128))
        pos3 = lax.broadcasted_iota(jnp.int32, (B, BLK, 128), 1).astype(F32)
        for s in range(NTP):
            cur = kall[c, s].astype(F32)
            kall[c, s] = jnp.where(pos3 + float(s * BLK) == len3, new3, cur).astype(BF16)

    def out_copy(c, s, ref):
        return pltpu.make_async_copy(kall.at[c, s], ref.at[:, pl.ds(s * BLK, BLK), :], sem_o.at[c, s])

    def x_copy(step, piece, n):
        sl = pl.ds(piece * NCH, NCH)
        return pltpu.make_async_remote_copy(
            src_ref=xown.at[step, :, sl], dst_ref=xrecv.at[step, me, :, sl],
            send_sem=send_x.at[step, piece, n], recv_sem=recv_x.at[step, me, piece],
            device_id={"tp": peers[n]}, device_id_type=MESH)

    def x_recv(step, piece, n):
        sl = pl.ds(piece * NCH, NCH)
        return pltpu.make_async_remote_copy(
            src_ref=xown.at[step, :, sl], dst_ref=xrecv.at[step, peers[n], :, sl],
            send_sem=send_x.at[step, piece, n], recv_sem=recv_x.at[step, peers[n], piece],
            device_id={"tp": peers[n]}, device_id_type=MESH)

    def x_send(step, piece, val):
        sl = pl.ds(piece * NCH, NCH)
        xown[step, :, sl] = val
        for n in range(3):
            x_copy(step, piece, n).start()
        xrecv[step, me, :, sl] = val

    def x_sum(step):
        for piece in range(D // NCH):
            for n in range(3):
                x_recv(step, piece, n).wait_recv()
        tot = xrecv[step, 0].astype(F32)
        for s in range(1, NTP):
            tot = tot + xrecv[step, s].astype(F32)
        return tot

    outs = (ok1_h, ov1_h, ok2_h, ov2_h)

    for l in range(2):
        a = _norm(h_f, ga[pl.ds(l, 1), :].astype(F32))
        qf = jnp.dot(a, wq[l], preferred_element_type=F32)
        kf = jnp.dot(a, wk[l], preferred_element_type=F32)
        vf = jnp.dot(a, wv[l], preferred_element_type=F32)
        q0 = _rope(qf[:, :128], cosv, sinv, low)
        q1 = _rope(qf[:, 128:], cosv, sinv, low)
        knew = _rope(kf, cosv, sinv, low).astype(BF16).astype(F32)
        vnew = vf.astype(BF16).astype(F32)
        zero = jnp.zeros_like(q0)
        qrows = jnp.concatenate([
            jnp.where(left, q0, zero), jnp.where(left, pltpu.roll(q0, 64, 1), zero),
            jnp.where(left, zero, pltpu.roll(q1, 64, 1)), jnp.where(left, zero, q1)], axis=0).astype(BF16)
        kc, vc = 2 * l, 2 * l + 1
        for n in range(3):
            cache_recv(kc, n).wait_recv()
        insert(kc, knew)
        for s in range(NTP):
            out_copy(kc, s, outs[kc]).start()
        k2d = kall[kc].reshape(NTP * B * BLK, 128)
        sc = lax.dot_general(qrows, k2d, (((1,), (1,)), ((), ())), preferred_element_type=F32) * 0.125
        sc = jnp.where(valid, sc, -1e30)
        ex = jnp.exp(sc - jnp.max(sc, axis=1, keepdims=True))
        prob = (ex / jnp.sum(ex, axis=1, keepdims=True)).astype(BF16)
        for n in range(3):
            cache_recv(vc, n).wait_recv()
        insert(vc, vnew)
        for s in range(NTP):
            out_copy(vc, s, outs[vc]).start()
        if l == 0:
            cache_copy(2, 0).start()
        v2d = kall[vc].reshape(NTP * B * BLK, 128)
        ov = jnp.dot(prob, v2d, preferred_element_type=F32)
        o0 = jnp.where(left, ov[0:16], pltpu.roll(ov[16:32], 64, 1))
        o1 = jnp.where(left, pltpu.roll(ov[32:48], 64, 1), ov[48:64])
        attn = jnp.concatenate([o0, o1], axis=1).astype(BF16)
        for piece in range(D // NCH):
            x_send(2 * l, piece, jnp.dot(attn, wo[l, :, pl.ds(piece * NCH, NCH)], preferred_element_type=F32).astype(BF16))
        h1 = (h_f + x_sum(2 * l)).astype(BF16).astype(F32)
        if l == 0:
            cache_copy(2, 1).start()
            cache_copy(3, 0).start()
        m = _norm(h1, gm[pl.ds(l, 1), :].astype(F32))

        lg = lax.dot_general(wr[l], m, (((1,), (1,)), ((), ())), preferred_element_type=F32)
        eid = lax.broadcasted_iota(jnp.int32, (EXP, B), 0)
        chosen = eid < 0
        for k in range(8):
            chosen = chosen | (cho[l, pl.ds(k, 1), :] == eid)
        lg = jnp.where(chosen, lg, -jnp.inf)
        ex = jnp.where(chosen, jnp.exp(lg - jnp.max(lg, axis=0, keepdims=True)), 0.0)
        gate_t = ex / jnp.sum(ex, axis=0, keepdims=True)
        gate = gate_t.T
        for e in range(EXP):
            gexp[e] = jnp.broadcast_to(gate[:, e:e + 1], (B, FL))

        def gate_up(i, _):
            g_copy(l, i).wait()
            u_copy(l, i).wait()
            for j in range(GCH):
                e = i * GCH + j
                w = jnp.concatenate([wg[l, e], wu[l, e]], axis=1)
                gu = jnp.dot(m, w, preferred_element_type=F32)
                g, u = gu[:, :FL], gu[:, FL:]
                act[e] = (g * jax.nn.sigmoid(g) * u * gexp[e]).astype(BF16)
            return 0
        lax.fori_loop(0, EXP // GCH, gate_up, 0)

        def dwait(i, _):
            d_copy(l, i).wait()
            return 0
        lax.fori_loop(0, EXP // DCH, dwait, 0)
        for piece in range(D // NCH):
            sl = pl.ds(piece * NCH, NCH)

            def down(i, acc):
                for j in range(4):
                    e = i * 8 + 2 * j
                    lhs = jnp.concatenate([act[e], act[e + 1]], axis=1)
                    rhs = jnp.concatenate([wd[l, e, :, sl], wd[l, e + 1, :, sl]], axis=0)
                    acc = acc + jnp.dot(lhs, rhs, preferred_element_type=F32)
                return acc
            acc = lax.fori_loop(0, EXP // 8, down, jnp.zeros((B, NCH), F32))
            x_send(2 * l + 1, piece, acc.astype(BF16))
        if l == 0:
            cache_copy(3, 1).start()
        h_f = (h1 + x_sum(2 * l + 1)).astype(BF16).astype(F32)

    hfin[...] = h_f.astype(BF16)
    done = pltpu.make_async_copy(hfin, hout_h, sem_s.at[0])
    done.start()
    for c in range(4):
        for s in range(NTP):
            out_copy(c, s, outs[c]).wait()
        for n in range(3):
            cache_copy(c, n).wait_send()
    for step in range(4):
        for piece in range(D // NCH):
            for n in range(3):
                x_copy(step, piece, n).wait_send()
    done.wait()


def solution(mesh):
    seq_spec = P('dp', 'tp', None, None)
    head_spec = P('dp', None, 'tp', None)
    col_spec = P(None, None, 'tp')
    ff_spec = P(None, None, None, 'tp')
    inv_freq = (THETA ** (-2.0 * np.arange(32, dtype=np.float64) / 64)).astype(np.float32)
    inv_row = np.tile(inv_freq, 4)[None, :]

    def local_step(hidden, lengths, choice, keys_one, vals_one, keys_two, vals_two, g_attn, w_q, w_k, w_v, w_o, g_mlp, w_router, w_gate, w_up, w_down):
        dense = jax.ShapeDtypeStruct((B, SEQ, 128), BF16)
        any_spec = pl.BlockSpec(memory_space=pl.ANY)
        V = pltpu.VMEM
        DMA = pltpu.SemaphoreType.DMA
        outs = pl.pallas_call(
            _kernel,
            out_shape=(jax.ShapeDtypeStruct((B, D), BF16), dense, dense, dense, dense),
            in_specs=[any_spec] * 18,
            out_specs=(any_spec,) * 5,
            scratch_shapes=[
                V((B, D), BF16), V((1, B), jnp.int32), V((2, 8, B), jnp.int32), V((4, B, BLK, 8, 64), BF16),
                V((2, D), BF16), V((2, D, 256), BF16), V((2, D, 128), BF16), V((2, D, 128), BF16), V((2, 256, D), BF16),
                V((2, D), BF16), V((2, EXP, D), BF16), V((2, EXP, D, FL), BF16), V((2, EXP, D, FL), BF16), V((2, EXP, FL, D), BF16),
                V((1, 128), F32),
                V((B * BLK * 8, 64), F32), V((4, NTP, B, BLK, 128), BF16), V((4, NTP, B, BLK, 128), BF16),
                V((4, B, D), BF16), V((4, NTP, B, D), BF16), V((EXP, B, FL), F32), V((EXP, B, FL), BF16), V((B, D), BF16),
                DMA((12,)), DMA((4,)), DMA((2, EXP // GCH)), DMA((2, EXP // GCH)), DMA((2, EXP // DCH)),
                DMA((4, 3)), DMA((4, NTP)), DMA((4, D // NCH, 3)), DMA((4, NTP, D // NCH)), DMA((4, NTP)),
            ],
            compiler_params=pltpu.CompilerParams(collective_id=0, has_side_effects=True, vmem_limit_bytes=66_900_000),
        )(hidden, lengths.reshape(1, B), jnp.transpose(choice, (0, 2, 1)), keys_one, vals_one, keys_two, vals_two,
          g_attn, w_q, w_k, w_v, w_o, g_mlp, jnp.transpose(w_router, (0, 2, 1)), w_gate, w_up, w_down, jnp.asarray(inv_row))
        return (outs[0],) + tuple(o.reshape(B, SEQ, 2, 64) for o in outs[1:])

    return jax.shard_map(local_step, mesh=mesh, in_specs=(P('dp', None), P('dp'), P(None, 'dp', None), seq_spec, seq_spec, seq_spec, seq_spec, P(), col_spec, col_spec, col_spec, P(None, 'tp', None), P(), P(), ff_spec, ff_spec, P(None, None, 'tp', None)), out_specs=(P('dp', None), head_spec, head_spec, head_spec, head_spec), check_vma=False)
```

time: 131 us -> 50.3 us (0.38)
  blocking collectives: 42.7 us -> 0 us
  Pallas kernels: 0 us -> 40 us
  matrix products: 33.4 us -> 0 us
  starting transfers between devices: 15 us -> 0 us
  other arithmetic: 12 us -> 0 us
  local copies, waits for them, and re-layouts: 17.6 us -> 9.35 us
  waiting for transfers between devices: 7.97 us -> 0 us
    psum x4 -> x0, blocking collectives: 42.7 us -> none  [the longest x2 22.1 us: decode_layer(): lax.psum(jnp.dot(attn_vec, w_o, preferred_element_type=jnp.float32).astyp...]
    pallas_call x0 -> x1, Pallas kernels: none -> 40 us  [local_step(): pl.pallas_call(_kernel, out_shape=(jax.ShapeDtypeStruct((B, D), BF16), de...]
    dot_general x18 -> x0, matrix products: 33.4 us -> none  [the longest x2 14.2 us: expert_block(): jnp.einsum('bef,efd->bd', expert_in, w_down, preferred_element_type=jnp.f...]
    all_to_all x4 -> x0, starting transfers between devices: 15 us -> none  [local_step(): lax.all_to_all(cache_blk, 'tp', 2, 1, tiled=True)]
    unnamed x26 -> x1, local copies, waits for them, and re-layouts: 10.3 us -> 1.37 us
    all_to_all x4 -> x0, waiting for transfers between devices: 7.97 us -> none  [local_step(): lax.all_to_all(cache_blk, 'tp', 2, 1, tiled=True)]
    reshape x2 -> x4, local copies, waits for them, and re-layouts: 0.18 us -> 7.98 us  [local_step(): return (outs[0],) + tuple((o.reshape(B, SEQ, 2, 64) for o in outs[1:]))]
    select_n x2 -> x0, other arithmetic: 3.9 us -> none  [decode_layer(): key_cache = jnp.where(is_new, key_new[:, None], key_cache)]
  transfers between devices with their start and end apart: 4 -> 0, of which waited for: 2 -> 0; matrix products, arithmetic and copies ran while one was open for 33% -> 0% of each run, Pallas kernels for 0% -> 0%
where the time goes in v1:
time: 50.3 us; the launch traced here: 50 us
  Pallas kernels  40 us (80%)
  local copies, waits for them, and re-layouts  9.35 us (19%)
  between operations  0.65 us (1%)
    pallas_call x1, Pallas kernels, local_step(): pl.pallas_call(_kernel, out_shape=(jax.ShapeDtypeStruct((B, D), BF16), de...  40 us
    reshape x4, local copies, waits for them, and re-layouts, local_step(): return (outs[0],) + tuple((o.reshape(B, SEQ, 2, 64) for o in outs[1:]))  7.98 us
    unnamed x1, local copies, waits for them, and re-layouts  1.37 us

profile of v1, /device:TPU:0, one launch (start us, length us, event | category | flops | bytes accessed | tf_op | source)
XLA Modules:
  0.0 50.0 jit_solution(5562996190194082387)
XLA Ops:
  0.6 40.0 %shard_map.209 = (bf16[16,1024]{1,0:T(8,128)(2,1)}, bf16[16,64,128]{2,1,0:T(8,128)(2,1)}, bf16[16,64,128]{2,1,0:T(8,128)(2,1)}, bf16[16,64,128]{2,1,0:T(8,128)(2,1)}, bf16[16,64,128]{2,1,0:T(8,128)(2,1)}) custom-call(bf16[16,1024]{1,0:T(8,128)(2,1)} %hid_h.1, s32[1,16]{1,0:T(1,128)} %bitcast.5, s32[2,8,16]{2,1,0:T(8,128)} %bitcast.4, ...), custom_call_target="tpu_custom_call" | custom-call | tf_op jit(solution)/shard_map/pallas_call | solution.py:311
  40.6 2.0 %reshape.26 = bf16[16,64,2,64]{3,2,1,0:T(2,128)(2,1)} reshape(bf16[16,64,128]{2,1,0:T(8,128)(2,1)} %get-tuple-element.11) | data formatting | bytes 524288 | tf_op jit(solution)/shard_map/reshape | solution.py:329
  42.6 2.0 %reshape.27 = bf16[16,64,2,64]{3,2,1,0:T(2,128)(2,1)} reshape(bf16[16,64,128]{2,1,0:T(8,128)(2,1)} %get-tuple-element.12) | data formatting | bytes 524288 | tf_op jit(solution)/shard_map/reshape | solution.py:329
  44.6 2.0 %reshape.28 = bf16[16,64,2,64]{3,2,1,0:T(2,128)(2,1)} reshape(bf16[16,64,128]{2,1,0:T(8,128)(2,1)} %get-tuple-element.13) | data formatting | bytes 524288 | tf_op jit(solution)/shard_map/reshape | solution.py:329
  46.6 2.0 %reshape.29 = bf16[16,64,2,64]{3,2,1,0:T(2,128)(2,1)} reshape(bf16[16,64,128]{2,1,0:T(8,128)(2,1)} %get-tuple-element.14) | data formatting | bytes 524288 | tf_op jit(solution)/shard_map/reshape | solution.py:329
  48.6 1.4 %copy.24 = bf16[16,1024]{1,0:T(8,128)(2,1)} copy(bf16[16,1024]{1,0:T(8,128)(2,1)} %get-tuple-element.20) | data formatting | bytes 65536

commit v2 on v1

--- a/solution.py
+++ b/solution.py
@@ -37,10 +37,10 @@
 
 
 def _kernel(hid_h, len_h, cho_h, k1_h, v1_h, k2_h, v2_h, ga_h, wq_h, wk_h, wv_h, wo_h, gm_h, wr_h, wg_h, wu_h, wd_h, inv_h,
-            hout_h, ok1_h, ov1_h, ok2_h, ov2_h,
+            hout, ok1, ov1, ok2, ov2,
             hid, lens, cho, raw, ga, wq, wk, wv, wo, gm, wr, wg, wu, wd, inv,
-            spread, snd, kall, xown, xrecv, gexp, act, hfin,
-            sem_s, sem_raw, sem_g, sem_u, sem_d, send_c, recv_c, send_x, recv_x, sem_o):
+            spread, snd, kall, xown, xrecv, gexp, act,
+            sem_s, sem_raw, sem_g, sem_u, sem_d, send_c, recv_c, send_x, recv_x):
     me = lax.axis_index("tp")
     chip, core = me // 2, me % 2
     partner = chip * 2 + (1 - core)
@@ -157,8 +157,12 @@
             cur = kall[c, s].astype(F32)
             kall[c, s] = jnp.where(pos3 + float(s * BLK) == len3, new3, cur).astype(BF16)
 
-    def out_copy(c, s, ref):
-        return pltpu.make_async_copy(kall.at[c, s], ref.at[:, pl.ds(s * BLK, BLK), :], sem_o.at[c, s])
+    def emit(c):
+        for s in range(NTP):
+            x = kall[c, s].reshape(B * BLK, 128).astype(F32)
+            spread[pl.ds(0, B * BLK, stride=2), :] = x[:, :64]
+            spread[pl.ds(1, B * BLK, stride=2), :] = x[:, 64:]
+            outs[c][:, pl.ds(s * 2 * BLK, 2 * BLK), :] = spread[pl.ds(0, 2 * B * BLK), :].astype(BF16).reshape(B, 2 * BLK, 64)
 
     def x_copy(step, piece, n):
         sl = pl.ds(piece * NCH, NCH)
@@ -190,7 +194,7 @@
             tot = tot + xrecv[step, s].astype(F32)
         return tot
 
-    outs = (ok1_h, ov1_h, ok2_h, ov2_h)
+    outs = (ok1, ov1, ok2, ov2)
 
     for l in range(2):
         a = _norm(h_f, ga[pl.ds(l, 1), :].astype(F32))
@@ -209,8 +213,6 @@
         for n in range(3):
             cache_recv(kc, n).wait_recv()
         insert(kc, knew)
-        for s in range(NTP):
-            out_copy(kc, s, outs[kc]).start()
         k2d = kall[kc].reshape(NTP * B * BLK, 128)
         sc = lax.dot_general(qrows, k2d, (((1,), (1,)), ((), ())), preferred_element_type=F32) * 0.125
         sc = jnp.where(valid, sc, -1e30)
@@ -219,8 +221,6 @@
         for n in range(3):
             cache_recv(vc, n).wait_recv()
         insert(vc, vnew)
-        for s in range(NTP):
-            out_copy(vc, s, outs[vc]).start()
         if l == 0:
             cache_copy(2, 0).start()
         v2d = kall[vc].reshape(NTP * B * BLK, 128)
@@ -230,6 +230,8 @@
         attn = jnp.concatenate([o0, o1], axis=1).astype(BF16)
         for piece in range(D // NCH):
             x_send(2 * l, piece, jnp.dot(attn, wo[l, :, pl.ds(piece * NCH, NCH)], preferred_element_type=F32).astype(BF16))
+        emit(kc)
+        emit(vc)
         h1 = (h_f + x_sum(2 * l)).astype(BF16).astype(F32)
         if l == 0:
             cache_copy(2, 1).start()
@@ -280,19 +282,23 @@
             cache_copy(3, 1).start()
         h_f = (h1 + x_sum(2 * l + 1)).astype(BF16).astype(F32)
 
-    hfin[...] = h_f.astype(BF16)
-    done = pltpu.make_async_copy(hfin, hout_h, sem_s.at[0])
-    done.start()
+    hout[...] = h_f.astype(BF16)
     for c in range(4):
-        for s in range(NTP):
-            out_copy(c, s, outs[c]).wait()
         for n in range(3):
             cache_copy(c, n).wait_send()
     for step in range(4):
         for piece in range(D // NCH):
             for n in range(3):
                 x_copy(step, piece, n).wait_send()
-    done.wait()
+
+
+def _store(h, k1, v1, k2, v2, ho, ok1, ov1, ok2, ov2, sem):
+    copies = [pltpu.make_async_copy(a, b, sem.at[i])
+              for i, (a, b) in enumerate(((k1, ok1), (v1, ov1), (k2, ok2), (v2, ov2), (h, ho)))]
+    for c in copies:
+        c.start()
+    for c in copies:
+        c.wait()
 
 
 def solution(mesh):
@@ -304,28 +310,36 @@
     inv_row = np.tile(inv_freq, 4)[None, :]
 
     def local_step(hidden, lengths, choice, keys_one, vals_one, keys_two, vals_two, g_attn, w_q, w_k, w_v, w_o, g_mlp, w_router, w_gate, w_up, w_down):
-        dense = jax.ShapeDtypeStruct((B, SEQ, 128), BF16)
+        shapes = (jax.ShapeDtypeStruct((B, D), BF16),) + (jax.ShapeDtypeStruct((B, 2 * SEQ, 64), BF16),) * 4
         any_spec = pl.BlockSpec(memory_space=pl.ANY)
+        vmem_spec = pl.BlockSpec(memory_space=pltpu.VMEM)
         V = pltpu.VMEM
         DMA = pltpu.SemaphoreType.DMA
         outs = pl.pallas_call(
             _kernel,
-            out_shape=(jax.ShapeDtypeStruct((B, D), BF16), dense, dense, dense, dense),
+            out_shape=tuple(V(s.shape, s.dtype) for s in shapes),
             in_specs=[any_spec] * 18,
-            out_specs=(any_spec,) * 5,
+            out_specs=(vmem_spec,) * 5,
             scratch_shapes=[
                 V((B, D), BF16), V((1, B), jnp.int32), V((2, 8, B), jnp.int32), V((4, B, BLK, 8, 64), BF16),
                 V((2, D), BF16), V((2, D, 256), BF16), V((2, D, 128), BF16), V((2, D, 128), BF16), V((2, 256, D), BF16),
                 V((2, D), BF16), V((2, EXP, D), BF16), V((2, EXP, D, FL), BF16), V((2, EXP, D, FL), BF16), V((2, EXP, FL, D), BF16),
                 V((1, 128), F32),
                 V((B * BLK * 8, 64), F32), V((4, NTP, B, BLK, 128), BF16), V((4, NTP, B, BLK, 128), BF16),
-                V((4, B, D), BF16), V((4, NTP, B, D), BF16), V((EXP, B, FL), F32), V((EXP, B, FL), BF16), V((B, D), BF16),
+                V((4, B, D), BF16), V((4, NTP, B, D), BF16), V((EXP, B, FL), F32), V((EXP, B, FL), BF16),
                 DMA((12,)), DMA((4,)), DMA((2, EXP // GCH)), DMA((2, EXP // GCH)), DMA((2, EXP // DCH)),
-                DMA((4, 3)), DMA((4, NTP)), DMA((4, D // NCH, 3)), DMA((4, NTP, D // NCH)), DMA((4, NTP)),
+                DMA((4, 3)), DMA((4, NTP)), DMA((4, D // NCH, 3)), DMA((4, NTP, D // NCH)),
             ],
-            compiler_params=pltpu.CompilerParams(collective_id=0, has_side_effects=True, vmem_limit_bytes=66_900_000),
+            compiler_params=pltpu.CompilerParams(collective_id=0, has_side_effects=True, vmem_limit_bytes=64_000_000),
         )(hidden, lengths.reshape(1, B), jnp.transpose(choice, (0, 2, 1)), keys_one, vals_one, keys_two, vals_two,
           g_attn, w_q, w_k, w_v, w_o, g_mlp, jnp.transpose(w_router, (0, 2, 1)), w_gate, w_up, w_down, jnp.asarray(inv_row))
+        outs = pl.pallas_call(
+            _store,
+            out_shape=shapes,
+            in_specs=[vmem_spec] * 5,
+            out_specs=(any_spec,) * 5,
+            scratch_shapes=[DMA((5,))],
+        )(*[pltpu.with_memory_space_constraint(o, pltpu.VMEM) for o in outs])
         return (outs[0],) + tuple(o.reshape(B, SEQ, 2, 64) for o in outs[1:])
 
     return jax.shard_map(local_step, mesh=mesh, in_specs=(P('dp', None), P('dp'), P(None, 'dp', None), seq_spec, seq_spec, seq_spec, seq_spec, P(), col_spec, col_spec, col_spec, P(None, 'tp', None), P(), P(), ff_spec, ff_spec, P(None, None, 'tp', None)), out_specs=(P('dp', None), head_spec, head_spec, head_spec, head_spec), check_vma=False)

time: 50.3 us -> 41.4 us (0.82)
  local copies, waits for them, and re-layouts: 9.35 us -> 0 us
  Pallas kernels: 40 us -> 40.6 us
    reshape x4 -> x0, local copies, waits for them, and re-layouts: 7.98 us -> none  [local_step(): return (outs[0],) + tuple((o.reshape(B, SEQ, 2, 64) for o in outs[1:]))]
    unnamed x1 -> x0, local copies, waits for them, and re-layouts: 1.37 us -> none
    pallas_call x1 -> x2, Pallas kernels: 40 us -> 40.6 us  [the longest x1 39.3 us: local_step(): pl.pallas_call(_kernel, out_shape=tuple((V(s.shape, s.dtype) for s in sha...]
where the time goes in v2:
time: 41.4 us; the launch traced here: 41.3 us
  Pallas kernels  40.6 us (98%)
  between operations  0.65 us (2%)
    pallas_call x1, Pallas kernels, local_step(): pl.pallas_call(_kernel, out_shape=tuple((V(s.shape, s.dtype) for s in sha...  39.3 us
    pallas_call x1, Pallas kernels, local_step(): pl.pallas_call(_store, out_shape=shapes, in_specs=[vmem_spec] * 5, out_sp...  1.36 us

profile of v2, /device:TPU:0, one launch (start us, length us, event | category | flops | bytes accessed | tf_op | source)
XLA Modules:
  0.0 41.3 jit_solution(14374933401623414772)
XLA Ops:
  0.6 39.3 %shard_map.209 = (bf16[16,1024]{1,0:T(8,128)(2,1)S(1)}, bf16[16,128,64]{2,1,0:T(8,128)(2,1)S(1)}, bf16[16,128,64]{2,1,0:T(8,128)(2,1)S(1)}, bf16[16,128,64]{2,1,0:T(8,128)(2,1)S(1)}, bf16[16,128,64]{2,1,0:T(8,128)(2,1)S(1)}) custom-call(bf16[16,1024]{1,0:T(8,128)(2,1)} %hid_h.1, s32[1,16]{1,0:T(1,128)} %bitcast.9, s32[2,8,16]{2,1,0:T(8,128)} %bitcast.8, ...), custom_call_target="tpu_custom_call" | custom-call | tf_op jit(solution)/shard_map/pallas_call | solution.py:318
  39.9 1.4 %shard_map.210 = (bf16[16,1024]{1,0:T(8,128)(2,1)}, bf16[16,128,64]{2,1,0:T(8,128)(2,1)}, bf16[16,128,64]{2,1,0:T(8,128)(2,1)}, bf16[16,128,64]{2,1,0:T(8,128)(2,1)}, bf16[16,128,64]{2,1,0:T(8,128)(2,1)}) custom-call(bf16[16,1024]{1,0:T(8,128)(2,1)S(1)} %get-tuple-element.15.h, bf16[16,128,64]{2,1,0:T(8,128)(2,1)S(1)} %get-tuple-element.16.k1, ...), custom_call_target="tpu_custom_call" | custom-call | tf_op jit(solution)/shard_map/pallas_call | solution.py:336

commit v3 on v2

--- a/solution.py
+++ b/solution.py
@@ -115,6 +115,8 @@
             snd[c, p] = jnp.concatenate([lo, hi], axis=1).astype(BF16).reshape(B, BLK, 128)
         kall[c, me] = snd[c, me]
 
+    start_layer(0)
+    start_layer(1)
     repack(0)
     pl.semaphore_wait(barrier, 3)
     for n in range(3):
@@ -122,8 +124,6 @@
     repack(1)
     for n in range(3):
         cache_copy(1, n).start()
-    start_layer(0)
-    start_layer(1)
     repack(2)
     repack(3)
     for c in (2, 3):

time: 41.4 us -> 41.4 us (level)
  no operation moved by 1% of the time
where the time goes in v3:
time: 41.4 us; the launch traced here: 41.3 us
  Pallas kernels  40.6 us (98%)
  between operations  0.65 us (2%)
    pallas_call x1, Pallas kernels, local_step(): pl.pallas_call(_kernel, out_shape=tuple((V(s.shape, s.dtype) for s in sha...  39.3 us
    pallas_call x1, Pallas kernels, local_step(): pl.pallas_call(_store, out_shape=shapes, in_specs=[vmem_spec] * 5, out_sp...  1.36 us

profile of v3, /device:TPU:0, one launch (start us, length us, event | category | flops | bytes accessed | tf_op | source)
XLA Modules:
  0.0 41.3 jit_solution(5242862501292423583)
XLA Ops:
  0.6 39.3 %shard_map.209 = (bf16[16,1024]{1,0:T(8,128)(2,1)S(1)}, bf16[16,128,64]{2,1,0:T(8,128)(2,1)S(1)}, bf16[16,128,64]{2,1,0:T(8,128)(2,1)S(1)}, bf16[16,128,64]{2,1,0:T(8,128)(2,1)S(1)}, bf16[16,128,64]{2,1,0:T(8,128)(2,1)S(1)}) custom-call(bf16[16,1024]{1,0:T(8,128)(2,1)} %hid_h.1, s32[1,16]{1,0:T(1,128)} %bitcast.9, s32[2,8,16]{2,1,0:T(8,128)} %bitcast.8, ...), custom_call_target="tpu_custom_call" | custom-call | tf_op jit(solution)/shard_map/pallas_call | solution.py:318
  39.9 1.4 %shard_map.210 = (bf16[16,1024]{1,0:T(8,128)(2,1)}, bf16[16,128,64]{2,1,0:T(8,128)(2,1)}, bf16[16,128,64]{2,1,0:T(8,128)(2,1)}, bf16[16,128,64]{2,1,0:T(8,128)(2,1)}, bf16[16,128,64]{2,1,0:T(8,128)(2,1)}) custom-call(bf16[16,1024]{1,0:T(8,128)(2,1)S(1)} %get-tuple-element.15.h, bf16[16,128,64]{2,1,0:T(8,128)(2,1)S(1)} %get-tuple-element.16.k1, ...), custom_call_target="tpu_custom_call" | custom-call | tf_op jit(solution)/shard_map/pallas_call | solution.py:336

commit v4 on v3

--- a/solution.py
+++ b/solution.py
@@ -21,7 +21,8 @@
 FL = 128
 GCH = 4
 DCH = 8
-NCH = 512
+PIECES = (((0, 1024),), ((0, 512), (512, 512)))
+NP = 2
 F32 = jnp.float32
 BF16 = jnp.bfloat16
 
@@ -39,7 +40,7 @@
 def _kernel(hid_h, len_h, cho_h, k1_h, v1_h, k2_h, v2_h, ga_h, wq_h, wk_h, wv_h, wo_h, gm_h, wr_h, wg_h, wu_h, wd_h, inv_h,
             hout, ok1, ov1, ok2, ov2,
             hid, lens, cho, raw, ga, wq, wk, wv, wo, gm, wr, wg, wu, wd, inv,
-            spread, snd, kall, xown, xrecv, gexp, act,
+            spread, snd, kall, xown, xrecv, act,
             sem_s, sem_raw, sem_g, sem_u, sem_d, send_c, recv_c, send_x, recv_x):
     me = lax.axis_index("tp")
     chip, core = me // 2, me % 2
@@ -145,50 +146,38 @@
     row = lax.broadcasted_iota(jnp.int32, (64, 1024), 0)
     len64 = jnp.concatenate([len_col] * 4, axis=0)
     pos = ((col // 256) * BLK + col % BLK).astype(F32)
-    valid = (((col // BLK) % B) == (row % B)) & (pos <= len64)
+    valid = (((col // BLK) % B) == (row % B)) & (pos < len64)
 
     h_f = hid[...].astype(F32)
 
-    def insert(c, new):
+    def emit(c, new):
         new3 = jnp.broadcast_to(new[:, None, :], (B, BLK, 128))
         len3 = jnp.broadcast_to(len_b[:, None, :], (B, BLK, 128))
         pos3 = lax.broadcasted_iota(jnp.int32, (B, BLK, 128), 1).astype(F32)
         for s in range(NTP):
-            cur = kall[c, s].astype(F32)
-            kall[c, s] = jnp.where(pos3 + float(s * BLK) == len3, new3, cur).astype(BF16)
-
-    def emit(c):
-        for s in range(NTP):
-            x = kall[c, s].reshape(B * BLK, 128).astype(F32)
+            x = jnp.where(pos3 + float(s * BLK) == len3, new3, kall[c, s].astype(F32)).reshape(B * BLK, 128)
             spread[pl.ds(0, B * BLK, stride=2), :] = x[:, :64]
             spread[pl.ds(1, B * BLK, stride=2), :] = x[:, 64:]
             outs[c][:, pl.ds(s * 2 * BLK, 2 * BLK), :] = spread[pl.ds(0, 2 * B * BLK), :].astype(BF16).reshape(B, 2 * BLK, 64)
 
-    def x_copy(step, piece, n):
-        sl = pl.ds(piece * NCH, NCH)
+    def x_desc(step, piece, n, slot):
+        sl = pl.ds(*PIECES[step % 2][piece])
         return pltpu.make_async_remote_copy(
-            src_ref=xown.at[step, :, sl], dst_ref=xrecv.at[step, me, :, sl],
-            send_sem=send_x.at[step, piece, n], recv_sem=recv_x.at[step, me, piece],
+            src_ref=xown.at[step, :, sl], dst_ref=xrecv.at[step, slot, :, sl],
+            send_sem=send_x.at[step, piece, n], recv_sem=recv_x.at[step, slot, piece],
             device_id={"tp": peers[n]}, device_id_type=MESH)
 
-    def x_recv(step, piece, n):
-        sl = pl.ds(piece * NCH, NCH)
-        return pltpu.make_async_remote_copy(
-            src_ref=xown.at[step, :, sl], dst_ref=xrecv.at[step, peers[n], :, sl],
-            send_sem=send_x.at[step, piece, n], recv_sem=recv_x.at[step, peers[n], piece],
-            device_id={"tp": peers[n]}, device_id_type=MESH)
-
     def x_send(step, piece, val):
-        sl = pl.ds(piece * NCH, NCH)
+        sl = pl.ds(*PIECES[step % 2][piece])
         xown[step, :, sl] = val
         for n in range(3):
-            x_copy(step, piece, n).start()
+            x_desc(step, piece, n, me).start()
         xrecv[step, me, :, sl] = val
 
     def x_sum(step):
-        for piece in range(D // NCH):
+        for piece in range(len(PIECES[step % 2])):
             for n in range(3):
-                x_recv(step, piece, n).wait_recv()
+                x_desc(step, piece, n, peers[n]).wait_recv()
         tot = xrecv[step, 0].astype(F32)
         for s in range(1, NTP):
             tot = tot + xrecv[step, s].astype(F32)
@@ -212,30 +201,30 @@
         kc, vc = 2 * l, 2 * l + 1
         for n in range(3):
             cache_recv(kc, n).wait_recv()
-        insert(kc, knew)
         k2d = kall[kc].reshape(NTP * B * BLK, 128)
         sc = lax.dot_general(qrows, k2d, (((1,), (1,)), ((), ())), preferred_element_type=F32) * 0.125
         sc = jnp.where(valid, sc, -1e30)
-        ex = jnp.exp(sc - jnp.max(sc, axis=1, keepdims=True))
-        prob = (ex / jnp.sum(ex, axis=1, keepdims=True)).astype(BF16)
+        ns = jnp.sum(qrows.astype(F32) * jnp.concatenate([knew] * 4, axis=0), axis=1, keepdims=True) * 0.125
+        top = jnp.maximum(jnp.max(sc, axis=1, keepdims=True), ns)
+        ex, nex = jnp.exp(sc - top), jnp.exp(ns - top)
+        den = jnp.sum(ex, axis=1, keepdims=True) + nex
+        prob = (ex / den).astype(BF16)
+        nprob = (nex / den).astype(BF16).astype(F32)
         for n in range(3):
             cache_recv(vc, n).wait_recv()
-        insert(vc, vnew)
-        if l == 0:
-            cache_copy(2, 0).start()
         v2d = kall[vc].reshape(NTP * B * BLK, 128)
-        ov = jnp.dot(prob, v2d, preferred_element_type=F32)
+        ov = jnp.dot(prob, v2d, preferred_element_type=F32) + nprob * jnp.concatenate([vnew] * 4, axis=0)
         o0 = jnp.where(left, ov[0:16], pltpu.roll(ov[16:32], 64, 1))
         o1 = jnp.where(left, pltpu.roll(ov[32:48], 64, 1), ov[48:64])
         attn = jnp.concatenate([o0, o1], axis=1).astype(BF16)
-        for piece in range(D // NCH):
-            x_send(2 * l, piece, jnp.dot(attn, wo[l, :, pl.ds(piece * NCH, NCH)], preferred_element_type=F32).astype(BF16))
-        emit(kc)
-        emit(vc)
-        h1 = (h_f + x_sum(2 * l)).astype(BF16).astype(F32)
+        x_send(2 * l, 0, jnp.dot(attn, wo[l], preferred_element_type=F32).astype(BF16))
         if l == 0:
+            cache_copy(2, 0).start()
             cache_copy(2, 1).start()
             cache_copy(3, 0).start()
+        emit(kc, knew)
+        emit(vc, vnew)
+        h1 = (h_f + x_sum(2 * l)).astype(BF16).astype(F32)
         m = _norm(h1, gm[pl.ds(l, 1), :].astype(F32))
 
         lg = lax.dot_general(wr[l], m, (((1,), (1,)), ((), ())), preferred_element_type=F32)
@@ -247,36 +236,21 @@
         ex = jnp.where(chosen, jnp.exp(lg - jnp.max(lg, axis=0, keepdims=True)), 0.0)
         gate_t = ex / jnp.sum(ex, axis=0, keepdims=True)
         gate = gate_t.T
-        for e in range(EXP):
-            gexp[e] = jnp.broadcast_to(gate[:, e:e + 1], (B, FL))
-
-        def gate_up(i, _):
+        for i in range(EXP // GCH):
             g_copy(l, i).wait()
             u_copy(l, i).wait()
-            for j in range(GCH):
-                e = i * GCH + j
-                w = jnp.concatenate([wg[l, e], wu[l, e]], axis=1)
-                gu = jnp.dot(m, w, preferred_element_type=F32)
-                g, u = gu[:, :FL], gu[:, FL:]
-                act[e] = (g * jax.nn.sigmoid(g) * u * gexp[e]).astype(BF16)
-            return 0
-        lax.fori_loop(0, EXP // GCH, gate_up, 0)
-
-        def dwait(i, _):
+        for i in range(EXP // DCH):
             d_copy(l, i).wait()
-            return 0
-        lax.fori_loop(0, EXP // DCH, dwait, 0)
-        for piece in range(D // NCH):
-            sl = pl.ds(piece * NCH, NCH)
-
-            def down(i, acc):
-                for j in range(4):
-                    e = i * 8 + 2 * j
-                    lhs = jnp.concatenate([act[e], act[e + 1]], axis=1)
-                    rhs = jnp.concatenate([wd[l, e, :, sl], wd[l, e + 1, :, sl]], axis=0)
-                    acc = acc + jnp.dot(lhs, rhs, preferred_element_type=F32)
-                return acc
-            acc = lax.fori_loop(0, EXP // 8, down, jnp.zeros((B, NCH), F32))
+        for e in range(EXP):
+            w = jnp.concatenate([wg[l, e], wu[l, e]], axis=1)
+            gu = jnp.dot(m, w, preferred_element_type=F32)
+            g, u = gu[:, :FL], gu[:, FL:]
+            act[:, pl.ds(e * FL, FL)] = (g * jax.nn.sigmoid(g) * u * jnp.broadcast_to(gate[:, e:e + 1], (B, FL))).astype(BF16)
+        for piece, (first, width) in enumerate(PIECES[1]):
+            acc = jnp.zeros((B, width), F32)
+            for e in range(0, EXP, 2):
+                rhs = wd[l, pl.ds(e, 2), :, pl.ds(first, width)].reshape(2 * FL, width)
+                acc = acc + jnp.dot(act[:, pl.ds(e * FL, 2 * FL)], rhs, preferred_element_type=F32)
             x_send(2 * l + 1, piece, acc.astype(BF16))
         if l == 0:
             cache_copy(3, 1).start()
@@ -287,9 +261,9 @@
         for n in range(3):
             cache_copy(c, n).wait_send()
     for step in range(4):
-        for piece in range(D // NCH):
+        for piece in range(len(PIECES[step % 2])):
             for n in range(3):
-                x_copy(step, piece, n).wait_send()
+                x_desc(step, piece, n, me).wait_send()
 
 
 def _store(h, k1, v1, k2, v2, ho, ok1, ov1, ok2, ov2, sem):
@@ -326,9 +300,9 @@
                 V((2, D), BF16), V((2, EXP, D), BF16), V((2, EXP, D, FL), BF16), V((2, EXP, D, FL), BF16), V((2, EXP, FL, D), BF16),
                 V((1, 128), F32),
                 V((B * BLK * 8, 64), F32), V((4, NTP, B, BLK, 128), BF16), V((4, NTP, B, BLK, 128), BF16),
-                V((4, B, D), BF16), V((4, NTP, B, D), BF16), V((EXP, B, FL), F32), V((EXP, B, FL), BF16),
+                V((4, B, D), BF16), V((4, NTP, B, D), BF16), V((B, EXP * FL), BF16),
                 DMA((12,)), DMA((4,)), DMA((2, EXP // GCH)), DMA((2, EXP // GCH)), DMA((2, EXP // DCH)),
-                DMA((4, 3)), DMA((4, NTP)), DMA((4, D // NCH, 3)), DMA((4, NTP, D // NCH)),
+                DMA((4, 3)), DMA((4, NTP)), DMA((4, NP, 3)), DMA((4, NTP, NP)),
             ],
             compiler_params=pltpu.CompilerParams(collective_id=0, has_side_effects=True, vmem_limit_bytes=64_000_000),
         )(hidden, lengths.reshape(1, B), jnp.transpose(choice, (0, 2, 1)), keys_one, vals_one, keys_two, vals_two,

time: 41.4 us -> 36.3 us (0.88)
  Pallas kernels: 40.6 us -> 35.6 us
    pallas_call x1, Pallas kernels: 39.3 us -> 34.2 us  [local_step(): pl.pallas_call(_kernel, out_shape=tuple((V(s.shape, s.dtype) for s in sha...]
where the time goes in v4:
time: 36.3 us; the launch traced here: 36.2 us
  Pallas kernels  35.6 us (98%)
  between operations  0.65 us (2%)
    pallas_call x1, Pallas kernels, local_step(): pl.pallas_call(_kernel, out_shape=tuple((V(s.shape, s.dtype) for s in sha...  34.2 us
    pallas_call x1, Pallas kernels, local_step(): pl.pallas_call(_store, out_shape=shapes, in_specs=[vmem_spec] * 5, out_sp...  1.36 us

profile of v4, /device:TPU:0, one launch (start us, length us, event | category | flops | bytes accessed | tf_op | source)
XLA Modules:
  0.0 36.2 jit_solution(15457293505971999982)
XLA Ops:
  0.6 34.2 %shard_map.209 = (bf16[16,1024]{1,0:T(8,128)(2,1)S(1)}, bf16[16,128,64]{2,1,0:T(8,128)(2,1)S(1)}, bf16[16,128,64]{2,1,0:T(8,128)(2,1)S(1)}, bf16[16,128,64]{2,1,0:T(8,128)(2,1)S(1)}, bf16[16,128,64]{2,1,0:T(8,128)(2,1)S(1)}) custom-call(bf16[16,1024]{1,0:T(8,128)(2,1)} %hid_h.1, s32[1,16]{1,0:T(1,128)} %bitcast.9, s32[2,8,16]{2,1,0:T(8,128)} %bitcast.8, ...), custom_call_target="tpu_custom_call" | custom-call | tf_op jit(solution)/shard_map/pallas_call | solution.py:292
  34.9 1.4 %shard_map.210 = (bf16[16,1024]{1,0:T(8,128)(2,1)}, bf16[16,128,64]{2,1,0:T(8,128)(2,1)}, bf16[16,128,64]{2,1,0:T(8,128)(2,1)}, bf16[16,128,64]{2,1,0:T(8,128)(2,1)}, bf16[16,128,64]{2,1,0:T(8,128)(2,1)}) custom-call(bf16[16,1024]{1,0:T(8,128)(2,1)S(1)} %get-tuple-element.15.h, bf16[16,128,64]{2,1,0:T(8,128)(2,1)S(1)} %get-tuple-element.16.k1, ...), custom_call_target="tpu_custom_call" | custom-call | tf_op jit(solution)/shard_map/pallas_call | solution.py:310

commit v5 on v4

--- a/solution.py
+++ b/solution.py
@@ -95,17 +95,24 @@
             return 0
         lax.fori_loop(0, EXP // DCH, dn, 0)
 
-    def cache_copy(c, n):
+    def cache_desc(c, n, part, slot):
+        rows = pl.ds(0, B) if part is None else pl.ds(part * (B // 2), B // 2)
+        k = part or 0
         return pltpu.make_async_remote_copy(
-            src_ref=snd.at[c, peers[n]], dst_ref=kall.at[c, me],
-            send_sem=send_c.at[c, n], recv_sem=recv_c.at[c, me],
+            src_ref=snd.at[c, peers[n], rows], dst_ref=kall.at[c, slot, rows],
+            send_sem=send_c.at[c, n, k], recv_sem=recv_c.at[c, slot, k],
             device_id={"tp": peers[n]}, device_id_type=MESH)
 
-    def cache_recv(c, n):
-        return pltpu.make_async_remote_copy(
-            src_ref=snd.at[c, peers[n]], dst_ref=kall.at[c, peers[n]],
-            send_sem=send_c.at[c, n], recv_sem=recv_c.at[c, peers[n]],
-            device_id={"tp": peers[n]}, device_id_type=MESH)
+    def parts(c, n):
+        return (0, 1) if (c, n) == (3, 1) else (None,)
+
+    def cache_copy(c, n, part=None):
+        return cache_desc(c, n, part, me)
+
+    def cache_wait(c):
+        for n in range(3):
+            for part in parts(c, n):
+                cache_desc(c, n, part, peers[n]).wait_recv()
 
     def repack(c):
         raw_copy(c).wait()
@@ -199,8 +206,7 @@
             jnp.where(left, q0, zero), jnp.where(left, pltpu.roll(q0, 64, 1), zero),
             jnp.where(left, zero, pltpu.roll(q1, 64, 1)), jnp.where(left, zero, q1)], axis=0).astype(BF16)
         kc, vc = 2 * l, 2 * l + 1
-        for n in range(3):
-            cache_recv(kc, n).wait_recv()
+        cache_wait(kc)
         k2d = kall[kc].reshape(NTP * B * BLK, 128)
         sc = lax.dot_general(qrows, k2d, (((1,), (1,)), ((), ())), preferred_element_type=F32) * 0.125
         sc = jnp.where(valid, sc, -1e30)
@@ -210,20 +216,24 @@
         den = jnp.sum(ex, axis=1, keepdims=True) + nex
         prob = (ex / den).astype(BF16)
         nprob = (nex / den).astype(BF16).astype(F32)
-        for n in range(3):
-            cache_recv(vc, n).wait_recv()
+        cache_wait(vc)
         v2d = kall[vc].reshape(NTP * B * BLK, 128)
         ov = jnp.dot(prob, v2d, preferred_element_type=F32) + nprob * jnp.concatenate([vnew] * 4, axis=0)
-        o0 = jnp.where(left, ov[0:16], pltpu.roll(ov[16:32], 64, 1))
-        o1 = jnp.where(left, pltpu.roll(ov[32:48], 64, 1), ov[48:64])
-        attn = jnp.concatenate([o0, o1], axis=1).astype(BF16)
-        x_send(2 * l, 0, jnp.dot(attn, wo[l], preferred_element_type=F32).astype(BF16))
+        attn = jnp.concatenate([jnp.where(left, ov[0:16], ov[48:64]), jnp.where(left, ov[16:32], ov[32:48])], axis=1).astype(BF16)
+        wo_rows = jnp.concatenate([wo[l, pl.ds(0, 64), :], wo[l, pl.ds(192, 64), :], wo[l, pl.ds(64, 128), :]], axis=0)
+        x_send(2 * l, 0, jnp.dot(attn, wo_rows, preferred_element_type=F32).astype(BF16))
         if l == 0:
             cache_copy(2, 0).start()
             cache_copy(2, 1).start()
             cache_copy(3, 0).start()
+            cache_copy(3, 1, 0).start()
         emit(kc, knew)
         emit(vc, vnew)
+        for i in range(EXP // GCH):
+            g_copy(l, i).wait()
+            u_copy(l, i).wait()
+        for i in range(EXP // DCH):
+            d_copy(l, i).wait()
         h1 = (h_f + x_sum(2 * l)).astype(BF16).astype(F32)
         m = _norm(h1, gm[pl.ds(l, 1), :].astype(F32))
 
@@ -236,30 +246,32 @@
         ex = jnp.where(chosen, jnp.exp(lg - jnp.max(lg, axis=0, keepdims=True)), 0.0)
         gate_t = ex / jnp.sum(ex, axis=0, keepdims=True)
         gate = gate_t.T
-        for i in range(EXP // GCH):
-            g_copy(l, i).wait()
-            u_copy(l, i).wait()
-        for i in range(EXP // DCH):
-            d_copy(l, i).wait()
         for e in range(EXP):
             w = jnp.concatenate([wg[l, e], wu[l, e]], axis=1)
             gu = jnp.dot(m, w, preferred_element_type=F32)
             g, u = gu[:, :FL], gu[:, FL:]
             act[:, pl.ds(e * FL, FL)] = (g * jax.nn.sigmoid(g) * u * jnp.broadcast_to(gate[:, e:e + 1], (B, FL))).astype(BF16)
-        for piece, (first, width) in enumerate(PIECES[1]):
-            acc = jnp.zeros((B, width), F32)
-            for e in range(0, EXP, 2):
+        def down(piece, pairs, acc):
+            first, width = PIECES[1][piece]
+            for e in pairs:
                 rhs = wd[l, pl.ds(e, 2), :, pl.ds(first, width)].reshape(2 * FL, width)
                 acc = acc + jnp.dot(act[:, pl.ds(e * FL, 2 * FL)], rhs, preferred_element_type=F32)
-            x_send(2 * l + 1, piece, acc.astype(BF16))
+            return acc
+
+        acc0 = down(0, range(0, EXP, 2), jnp.zeros((B, PIECES[1][0][1]), F32))
+        acc1 = down(1, range(0, 8, 2), jnp.zeros((B, PIECES[1][1][1]), F32))
+        x_send(2 * l + 1, 0, acc0.astype(BF16))
+        acc1 = down(1, range(8, EXP, 2), acc1)
+        x_send(2 * l + 1, 1, acc1.astype(BF16))
         if l == 0:
-            cache_copy(3, 1).start()
+            cache_copy(3, 1, 1).start()
         h_f = (h1 + x_sum(2 * l + 1)).astype(BF16).astype(F32)
 
     hout[...] = h_f.astype(BF16)
     for c in range(4):
         for n in range(3):
-            cache_copy(c, n).wait_send()
+            for part in parts(c, n):
+                cache_copy(c, n, part).wait_send()
     for step in range(4):
         for piece in range(len(PIECES[step % 2])):
             for n in range(3):
@@ -302,7 +314,7 @@
                 V((B * BLK * 8, 64), F32), V((4, NTP, B, BLK, 128), BF16), V((4, NTP, B, BLK, 128), BF16),
                 V((4, B, D), BF16), V((4, NTP, B, D), BF16), V((B, EXP * FL), BF16),
                 DMA((12,)), DMA((4,)), DMA((2, EXP // GCH)), DMA((2, EXP // GCH)), DMA((2, EXP // DCH)),
-                DMA((4, 3)), DMA((4, NTP)), DMA((4, NP, 3)), DMA((4, NTP, NP)),
+                DMA((4, 3, 2)), DMA((4, NTP, 2)), DMA((4, NP, 3)), DMA((4, NTP, NP)),
             ],
             compiler_params=pltpu.CompilerParams(collective_id=0, has_side_effects=True, vmem_limit_bytes=64_000_000),
         )(hidden, lengths.reshape(1, B), jnp.transpose(choice, (0, 2, 1)), keys_one, vals_one, keys_two, vals_two,

time: 36.3 us -> 36 us (level)
  no operation moved by 1% of the time
where the time goes in v5:
time: 36 us; the launch traced here: 35.9 us
  Pallas kernels  35.3 us (98%)
  between operations  0.65 us (2%)
    pallas_call x1, Pallas kernels, local_step(): pl.pallas_call(_kernel, out_shape=tuple((V(s.shape, s.dtype) for s in sha...  33.9 us
    pallas_call x1, Pallas kernels, local_step(): pl.pallas_call(_store, out_shape=shapes, in_specs=[vmem_spec] * 5, out_sp...  1.36 us

profile of v5, /device:TPU:0, one launch (start us, length us, event | category | flops | bytes accessed | tf_op | source)
XLA Modules:
  0.0 35.9 jit_solution(5238151420721291279)
XLA Ops:
  0.6 33.9 %shard_map.209 = (bf16[16,1024]{1,0:T(8,128)(2,1)S(1)}, bf16[16,128,64]{2,1,0:T(8,128)(2,1)S(1)}, bf16[16,128,64]{2,1,0:T(8,128)(2,1)S(1)}, bf16[16,128,64]{2,1,0:T(8,128)(2,1)S(1)}, bf16[16,128,64]{2,1,0:T(8,128)(2,1)S(1)}) custom-call(bf16[16,1024]{1,0:T(8,128)(2,1)} %hid_h.1, s32[1,16]{1,0:T(1,128)} %bitcast.9, s32[2,8,16]{2,1,0:T(8,128)} %bitcast.8, ...), custom_call_target="tpu_custom_call" | custom-call | tf_op jit(solution)/shard_map/pallas_call | solution.py:304
  34.6 1.4 %shard_map.210 = (bf16[16,1024]{1,0:T(8,128)(2,1)}, bf16[16,128,64]{2,1,0:T(8,128)(2,1)}, bf16[16,128,64]{2,1,0:T(8,128)(2,1)}, bf16[16,128,64]{2,1,0:T(8,128)(2,1)}, bf16[16,128,64]{2,1,0:T(8,128)(2,1)}) custom-call(bf16[16,1024]{1,0:T(8,128)(2,1)S(1)} %get-tuple-element.15.h, bf16[16,128,64]{2,1,0:T(8,128)(2,1)S(1)} %get-tuple-element.16.k1, ...), custom_call_target="tpu_custom_call" | custom-call | tf_op jit(solution)/shard_map/pallas_call | solution.py:322

commit v6 on v5

--- a/solution.py
+++ b/solution.py
@@ -104,7 +104,7 @@
             device_id={"tp": peers[n]}, device_id_type=MESH)
 
     def parts(c, n):
-        return (0, 1) if (c, n) == (3, 1) else (None,)
+        return (None,)
 
     def cache_copy(c, n, part=None):
         return cache_desc(c, n, part, me)
@@ -124,7 +124,6 @@
         kall[c, me] = snd[c, me]
 
     start_layer(0)
-    start_layer(1)
     repack(0)
     pl.semaphore_wait(barrier, 3)
     for n in range(3):
@@ -133,9 +132,10 @@
     for n in range(3):
         cache_copy(1, n).start()
     repack(2)
+    cache_copy(2, 0).start()
+    cache_copy(2, 2).start()
     repack(3)
-    for c in (2, 3):
-        cache_copy(c, 2).start()
+    cache_copy(3, 2).start()
 
     for i in range(len(smalls)):
         small_copy(i).wait()
@@ -223,10 +223,9 @@
         wo_rows = jnp.concatenate([wo[l, pl.ds(0, 64), :], wo[l, pl.ds(192, 64), :], wo[l, pl.ds(64, 128), :]], axis=0)
         x_send(2 * l, 0, jnp.dot(attn, wo_rows, preferred_element_type=F32).astype(BF16))
         if l == 0:
-            cache_copy(2, 0).start()
             cache_copy(2, 1).start()
             cache_copy(3, 0).start()
-            cache_copy(3, 1, 0).start()
+            cache_copy(3, 1).start()
         emit(kc, knew)
         emit(vc, vnew)
         for i in range(EXP // GCH):
@@ -234,6 +233,8 @@
             u_copy(l, i).wait()
         for i in range(EXP // DCH):
             d_copy(l, i).wait()
+        if l == 0:
+            start_layer(1)
         h1 = (h_f + x_sum(2 * l)).astype(BF16).astype(F32)
         m = _norm(h1, gm[pl.ds(l, 1), :].astype(F32))
 
@@ -263,8 +264,6 @@
         x_send(2 * l + 1, 0, acc0.astype(BF16))
         acc1 = down(1, range(8, EXP, 2), acc1)
         x_send(2 * l + 1, 1, acc1.astype(BF16))
-        if l == 0:
-            cache_copy(3, 1, 1).start()
         h_f = (h1 + x_sum(2 * l + 1)).astype(BF16).astype(F32)
 
     hout[...] = h_f.astype(BF16)

time: 36 us -> 36.1 us (level)
  no operation moved by 1% of the time
where the time goes in v6:
time: 36.1 us; the launch traced here: 36 us
  Pallas kernels  35.4 us (98%)
  between operations  0.65 us (2%)
    pallas_call x1, Pallas kernels, local_step(): pl.pallas_call(_kernel, out_shape=tuple((V(s.shape, s.dtype) for s in sha...  34 us
    pallas_call x1, Pallas kernels, local_step(): pl.pallas_call(_store, out_shape=shapes, in_specs=[vmem_spec] * 5, out_sp...  1.36 us

profile of v6, /device:TPU:0, one launch (start us, length us, event | category | flops | bytes accessed | tf_op | source)
XLA Modules:
  0.0 36.0 jit_solution(13099636870044912961)
XLA Ops:
  0.6 34.0 %shard_map.209 = (bf16[16,1024]{1,0:T(8,128)(2,1)S(1)}, bf16[16,128,64]{2,1,0:T(8,128)(2,1)S(1)}, bf16[16,128,64]{2,1,0:T(8,128)(2,1)S(1)}, bf16[16,128,64]{2,1,0:T(8,128)(2,1)S(1)}, bf16[16,128,64]{2,1,0:T(8,128)(2,1)S(1)}) custom-call(bf16[16,1024]{1,0:T(8,128)(2,1)} %hid_h.1, s32[1,16]{1,0:T(1,128)} %bitcast.9, s32[2,8,16]{2,1,0:T(8,128)} %bitcast.8, ...), custom_call_target="tpu_custom_call" | custom-call | tf_op jit(solution)/shard_map/pallas_call | solution.py:303
  34.7 1.4 %shard_map.210 = (bf16[16,1024]{1,0:T(8,128)(2,1)}, bf16[16,128,64]{2,1,0:T(8,128)(2,1)}, bf16[16,128,64]{2,1,0:T(8,128)(2,1)}, bf16[16,128,64]{2,1,0:T(8,128)(2,1)}, bf16[16,128,64]{2,1,0:T(8,128)(2,1)}) custom-call(bf16[16,1024]{1,0:T(8,128)(2,1)S(1)} %get-tuple-element.15.h, bf16[16,128,64]{2,1,0:T(8,128)(2,1)S(1)} %get-tuple-element.16.k1, ...), custom_call_target="tpu_custom_call" | custom-call | tf_op jit(solution)/shard_map/pallas_call | solution.py:321

commit v7 on v6

--- a/solution.py
+++ b/solution.py
@@ -54,6 +54,7 @@
         pl.semaphore_signal(barrier, inc=1, device_id={"tp": p}, device_id_type=MESH)
 
     raw_src = (k1_h, v1_h, k2_h, v2_h)
+    pending = {}
 
     def raw_copy(c):
         return pltpu.make_async_copy(raw_src[c], raw.at[c], sem_raw.at[c])
@@ -84,38 +85,31 @@
     raw_copy(3).start()
 
     def start_layer(l):
-        def gu(i, _):
+        for i in range(EXP // GCH):
             g_copy(l, i).start()
             u_copy(l, i).start()
-            return 0
-        lax.fori_loop(0, EXP // GCH, gu, 0)
-
-        def dn(i, _):
+            pending["g", l, i] = g_copy(l, i).wait
+            pending["u", l, i] = u_copy(l, i).wait
+        for i in range(EXP // DCH):
             d_copy(l, i).start()
-            return 0
-        lax.fori_loop(0, EXP // DCH, dn, 0)
-
-    def cache_desc(c, n, part, slot):
-        rows = pl.ds(0, B) if part is None else pl.ds(part * (B // 2), B // 2)
-        k = part or 0
+            pending["d", l, i] = d_copy(l, i).wait
+
+    def finish(*prefix):
+        for key in [k for k in pending if k[:len(prefix)] == prefix]:
+            pending.pop(key)()
+
+    def cache_desc(c, n, slot):
         return pltpu.make_async_remote_copy(
-            src_ref=snd.at[c, peers[n], rows], dst_ref=kall.at[c, slot, rows],
-            send_sem=send_c.at[c, n, k], recv_sem=recv_c.at[c, slot, k],
+            src_ref=snd.at[c, peers[n]], dst_ref=kall.at[c, slot],
+            send_sem=send_c.at[c, n], recv_sem=recv_c.at[c, slot],
             device_id={"tp": peers[n]}, device_id_type=MESH)
 
-    def parts(c, n):
-        return (None,)
-
-    def cache_copy(c, n, part=None):
-        return cache_desc(c, n, part, me)
-
-    def cache_wait(c):
-        for n in range(3):
-            for part in parts(c, n):
-                cache_desc(c, n, part, peers[n]).wait_recv()
+    def cache_send(c, n):
+        cache_desc(c, n, me).start()
+        pending["cs", c, n] = cache_desc(c, n, me).wait_send
+        pending["cr", c, n] = cache_desc(c, n, peers[n]).wait_recv
 
     def repack(c):
-        raw_copy(c).wait()
         spread[...] = raw[c].reshape(B * BLK * 8, 64).astype(F32)
         for p in range(NTP):
             lo = spread[pl.ds(2 * p, B * BLK, stride=8), :]
@@ -123,22 +117,26 @@
             snd[c, p] = jnp.concatenate([lo, hi], axis=1).astype(BF16).reshape(B, BLK, 128)
         kall[c, me] = snd[c, me]
 
-    start_layer(0)
+    raw_copy(0).wait()
     repack(0)
     pl.semaphore_wait(barrier, 3)
     for n in range(3):
-        cache_copy(0, n).start()
+        cache_send(0, n)
+    raw_copy(1).wait()
     repack(1)
     for n in range(3):
-        cache_copy(1, n).start()
-    repack(2)
-    cache_copy(2, 0).start()
-    cache_copy(2, 2).start()
-    repack(3)
-    cache_copy(3, 2).start()
-
+        cache_send(1, n)
     for i in range(len(smalls)):
         small_copy(i).wait()
+    raw_copy(2).wait()
+    raw_copy(3).wait()
+    start_layer(0)
+    repack(2)
+    cache_send(2, 0)
+    cache_send(2, 2)
+    repack(3)
+    cache_send(3, 2)
+
 
     eye = lax.broadcasted_iota(jnp.int32, (B, B), 0) == lax.broadcasted_iota(jnp.int32, (B, B), 1)
     len_row = jnp.broadcast_to(lens[...].astype(F32), (B, B))
@@ -179,12 +177,12 @@
         xown[step, :, sl] = val
         for n in range(3):
             x_desc(step, piece, n, me).start()
+            pending["xs", step, piece, n] = x_desc(step, piece, n, me).wait_send
+            pending["xr", step, piece, n] = x_desc(step, piece, n, peers[n]).wait_recv
         xrecv[step, me, :, sl] = val
 
     def x_sum(step):
-        for piece in range(len(PIECES[step % 2])):
-            for n in range(3):
-                x_desc(step, piece, n, peers[n]).wait_recv()
+        finish("xr", step)
         tot = xrecv[step, 0].astype(F32)
         for s in range(1, NTP):
             tot = tot + xrecv[step, s].astype(F32)
@@ -206,7 +204,7 @@
             jnp.where(left, q0, zero), jnp.where(left, pltpu.roll(q0, 64, 1), zero),
             jnp.where(left, zero, pltpu.roll(q1, 64, 1)), jnp.where(left, zero, q1)], axis=0).astype(BF16)
         kc, vc = 2 * l, 2 * l + 1
-        cache_wait(kc)
+        finish("cr", kc)
         k2d = kall[kc].reshape(NTP * B * BLK, 128)
         sc = lax.dot_general(qrows, k2d, (((1,), (1,)), ((), ())), preferred_element_type=F32) * 0.125
         sc = jnp.where(valid, sc, -1e30)
@@ -216,23 +214,20 @@
         den = jnp.sum(ex, axis=1, keepdims=True) + nex
         prob = (ex / den).astype(BF16)
         nprob = (nex / den).astype(BF16).astype(F32)
-        cache_wait(vc)
+        finish("cr", vc)
         v2d = kall[vc].reshape(NTP * B * BLK, 128)
         ov = jnp.dot(prob, v2d, preferred_element_type=F32) + nprob * jnp.concatenate([vnew] * 4, axis=0)
         attn = jnp.concatenate([jnp.where(left, ov[0:16], ov[48:64]), jnp.where(left, ov[16:32], ov[32:48])], axis=1).astype(BF16)
         wo_rows = jnp.concatenate([wo[l, pl.ds(0, 64), :], wo[l, pl.ds(192, 64), :], wo[l, pl.ds(64, 128), :]], axis=0)
         x_send(2 * l, 0, jnp.dot(attn, wo_rows, preferred_element_type=F32).astype(BF16))
         if l == 0:
-            cache_copy(2, 1).start()
-            cache_copy(3, 0).start()
-            cache_copy(3, 1).start()
+            cache_send(2, 1)
+            cache_send(3, 0)
+            cache_send(3, 1)
         emit(kc, knew)
         emit(vc, vnew)
-        for i in range(EXP // GCH):
-            g_copy(l, i).wait()
-            u_copy(l, i).wait()
-        for i in range(EXP // DCH):
-            d_copy(l, i).wait()
+        for kind in "gud":
+            finish(kind, l)
         if l == 0:
             start_layer(1)
         h1 = (h_f + x_sum(2 * l)).astype(BF16).astype(F32)
@@ -267,14 +262,7 @@
         h_f = (h1 + x_sum(2 * l + 1)).astype(BF16).astype(F32)
 
     hout[...] = h_f.astype(BF16)
-    for c in range(4):
-        for n in range(3):
-            for part in parts(c, n):
-                cache_copy(c, n, part).wait_send()
-    for step in range(4):
-        for piece in range(len(PIECES[step % 2])):
-            for n in range(3):
-                x_desc(step, piece, n, me).wait_send()
+    finish()
 
 
 def _store(h, k1, v1, k2, v2, ho, ok1, ov1, ok2, ov2, sem):
@@ -313,7 +301,7 @@
                 V((B * BLK * 8, 64), F32), V((4, NTP, B, BLK, 128), BF16), V((4, NTP, B, BLK, 128), BF16),
                 V((4, B, D), BF16), V((4, NTP, B, D), BF16), V((B, EXP * FL), BF16),
                 DMA((12,)), DMA((4,)), DMA((2, EXP // GCH)), DMA((2, EXP // GCH)), DMA((2, EXP // DCH)),
-                DMA((4, 3, 2)), DMA((4, NTP, 2)), DMA((4, NP, 3)), DMA((4, NTP, NP)),
+                DMA((4, 3)), DMA((4, NTP)), DMA((4, NP, 3)), DMA((4, NTP, NP)),
             ],
             compiler_params=pltpu.CompilerParams(collective_id=0, has_side_effects=True, vmem_limit_bytes=64_000_000),
         )(hidden, lengths.reshape(1, B), jnp.transpose(choice, (0, 2, 1)), keys_one, vals_one, keys_two, vals_two,

time: 36.1 us -> 35.9 us (level)
  no operation moved by 1% of the time
where the time goes in v7:
time: 35.9 us; the launch traced here: 35.8 us
  Pallas kernels  35.1 us (98%)
  between operations  0.65 us (2%)
    pallas_call x1, Pallas kernels, local_step(): pl.pallas_call(_kernel, out_shape=tuple((V(s.shape, s.dtype) for s in sha...  33.8 us
    pallas_call x1, Pallas kernels, local_step(): pl.pallas_call(_store, out_shape=shapes, in_specs=[vmem_spec] * 5, out_sp...  1.36 us

profile of v7, /device:TPU:0, one launch (start us, length us, event | category | flops | bytes accessed | tf_op | source)
XLA Modules:
  0.0 35.8 jit_solution(10138720253288982580)
XLA Ops:
  0.6 33.8 %shard_map.209 = (bf16[16,1024]{1,0:T(8,128)(2,1)S(1)}, bf16[16,128,64]{2,1,0:T(8,128)(2,1)S(1)}, bf16[16,128,64]{2,1,0:T(8,128)(2,1)S(1)}, bf16[16,128,64]{2,1,0:T(8,128)(2,1)S(1)}, bf16[16,128,64]{2,1,0:T(8,128)(2,1)S(1)}) custom-call(bf16[16,1024]{1,0:T(8,128)(2,1)} %hid_h.1, s32[1,16]{1,0:T(1,128)} %bitcast.9, s32[2,8,16]{2,1,0:T(8,128)} %bitcast.8, ...), custom_call_target="tpu_custom_call" | custom-call | tf_op jit(solution)/shard_map/pallas_call | solution.py:291
  34.4 1.4 %shard_map.210 = (bf16[16,1024]{1,0:T(8,128)(2,1)}, bf16[16,128,64]{2,1,0:T(8,128)(2,1)}, bf16[16,128,64]{2,1,0:T(8,128)(2,1)}, bf16[16,128,64]{2,1,0:T(8,128)(2,1)}, bf16[16,128,64]{2,1,0:T(8,128)(2,1)}) custom-call(bf16[16,1024]{1,0:T(8,128)(2,1)S(1)} %get-tuple-element.15.h, bf16[16,128,64]{2,1,0:T(8,128)(2,1)S(1)} %get-tuple-element.16.k1, ...), custom_call_target="tpu_custom_call" | custom-call | tf_op jit(solution)/shard_map/pallas_call | solution.py:309

commit v8 on v7

--- a/solution.py
+++ b/solution.py
@@ -79,10 +79,6 @@
 
     raw_copy(0).start()
     raw_copy(1).start()
-    for i in range(len(smalls)):
-        small_copy(i).start()
-    raw_copy(2).start()
-    raw_copy(3).start()
 
     def start_layer(l):
         for i in range(EXP // GCH):
@@ -118,11 +114,15 @@
         kall[c, me] = snd[c, me]
 
     raw_copy(0).wait()
+    for i in range(len(smalls)):
+        small_copy(i).start()
     repack(0)
     pl.semaphore_wait(barrier, 3)
     for n in range(3):
         cache_send(0, n)
     raw_copy(1).wait()
+    raw_copy(2).start()
+    raw_copy(3).start()
     repack(1)
     for n in range(3):
         cache_send(1, n)

time: 35.9 us -> 35.5 us (0.989)
  Pallas kernels: 35.1 us -> 34.7 us
    pallas_call x1, Pallas kernels: 33.8 us -> 33.4 us  [local_step(): pl.pallas_call(_kernel, out_shape=tuple((V(s.shape, s.dtype) for s in sha...]
where the time goes in v8:
time: 35.5 us; the launch traced here: 35.4 us
  Pallas kernels  34.7 us (98%)
  between operations  0.65 us (2%)
    pallas_call x1, Pallas kernels, local_step(): pl.pallas_call(_kernel, out_shape=tuple((V(s.shape, s.dtype) for s in sha...  33.4 us
    pallas_call x1, Pallas kernels, local_step(): pl.pallas_call(_store, out_shape=shapes, in_specs=[vmem_spec] * 5, out_sp...  1.36 us

profile of v8, /device:TPU:0, one launch (start us, length us, event | category | flops | bytes accessed | tf_op | source)
XLA Modules:
  0.0 35.4 jit_solution(2151943921360811665)
XLA Ops:
  0.6 33.4 %shard_map.209 = (bf16[16,1024]{1,0:T(8,128)(2,1)S(1)}, bf16[16,128,64]{2,1,0:T(8,128)(2,1)S(1)}, bf16[16,128,64]{2,1,0:T(8,128)(2,1)S(1)}, bf16[16,128,64]{2,1,0:T(8,128)(2,1)S(1)}, bf16[16,128,64]{2,1,0:T(8,128)(2,1)S(1)}) custom-call(bf16[16,1024]{1,0:T(8,128)(2,1)} %hid_h.1, s32[1,16]{1,0:T(1,128)} %bitcast.9, s32[2,8,16]{2,1,0:T(8,128)} %bitcast.8, ...), custom_call_target="tpu_custom_call" | custom-call | tf_op jit(solution)/shard_map/pallas_call | solution.py:291
  34.0 1.4 %shard_map.210 = (bf16[16,1024]{1,0:T(8,128)(2,1)}, bf16[16,128,64]{2,1,0:T(8,128)(2,1)}, bf16[16,128,64]{2,1,0:T(8,128)(2,1)}, bf16[16,128,64]{2,1,0:T(8,128)(2,1)}, bf16[16,128,64]{2,1,0:T(8,128)(2,1)}) custom-call(bf16[16,1024]{1,0:T(8,128)(2,1)S(1)} %get-tuple-element.15.h, bf16[16,128,64]{2,1,0:T(8,128)(2,1)S(1)} %get-tuple-element.16.k1, ...), custom_call_target="tpu_custom_call" | custom-call | tf_op jit(solution)/shard_map/pallas_call | solution.py:309

commit v9 on v8

--- a/solution.py
+++ b/solution.py
@@ -41,7 +41,7 @@
             hout, ok1, ov1, ok2, ov2,
             hid, lens, cho, raw, ga, wq, wk, wv, wo, gm, wr, wg, wu, wd, inv,
             spread, snd, kall, xown, xrecv, act,
-            sem_s, sem_raw, sem_g, sem_u, sem_d, send_c, recv_c, send_x, recv_x):
+            sem_s, sem_raw, sem_w, send_c, recv_c, send_x, recv_x):
     me = lax.axis_index("tp")
     chip, core = me // 2, me % 2
     partner = chip * 2 + (1 - core)
@@ -54,7 +54,6 @@
         pl.semaphore_signal(barrier, inc=1, device_id={"tp": p}, device_id_type=MESH)
 
     raw_src = (k1_h, v1_h, k2_h, v2_h)
-    pending = {}
 
     def raw_copy(c):
         return pltpu.make_async_copy(raw_src[c], raw.at[c], sem_raw.at[c])
@@ -65,45 +64,28 @@
     def small_copy(i):
         return pltpu.make_async_copy(smalls[i][0], smalls[i][1], sem_s.at[i])
 
-    def g_copy(l, i):
-        sl = pl.ds(i * GCH, GCH)
-        return pltpu.make_async_copy(wg_h.at[l, sl], wg.at[l, sl], sem_g.at[l, i])
-
-    def u_copy(l, i):
-        sl = pl.ds(i * GCH, GCH)
-        return pltpu.make_async_copy(wu_h.at[l, sl], wu.at[l, sl], sem_u.at[l, i])
-
-    def d_copy(l, i):
-        sl = pl.ds(i * DCH, DCH)
-        return pltpu.make_async_copy(wd_h.at[l, sl], wd.at[l, sl], sem_d.at[l, i])
+    def w_copy(l, k):
+        src, dst = ((wg_h, wg), (wu_h, wu), (wd_h, wd))[k]
+        return pltpu.make_async_copy(src.at[l], dst.at[l], sem_w.at[l, k])
 
     raw_copy(0).start()
     raw_copy(1).start()
 
     def start_layer(l):
-        for i in range(EXP // GCH):
-            g_copy(l, i).start()
-            u_copy(l, i).start()
-            pending["g", l, i] = g_copy(l, i).wait
-            pending["u", l, i] = u_copy(l, i).wait
-        for i in range(EXP // DCH):
-            d_copy(l, i).start()
-            pending["d", l, i] = d_copy(l, i).wait
-
-    def finish(*prefix):
-        for key in [k for k in pending if k[:len(prefix)] == prefix]:
-            pending.pop(key)()
-
-    def cache_desc(c, n, slot):
-        return pltpu.make_async_remote_copy(
-            src_ref=snd.at[c, peers[n]], dst_ref=kall.at[c, slot],
-            send_sem=send_c.at[c, n], recv_sem=recv_c.at[c, slot],
-            device_id={"tp": peers[n]}, device_id_type=MESH)
+        for k in range(3):
+            w_copy(l, k).start()
 
     def cache_send(c, n):
-        cache_desc(c, n, me).start()
-        pending["cs", c, n] = cache_desc(c, n, me).wait_send
-        pending["cr", c, n] = cache_desc(c, n, peers[n]).wait_recv
+        pltpu.make_async_remote_copy(
+            src_ref=snd.at[c, peers[n]], dst_ref=kall.at[c, me],
+            send_sem=send_c.at[0], recv_sem=recv_c.at[c],
+            device_id={"tp": peers[n]}, device_id_type=MESH).start()
+
+    def cache_wait(c):
+        pltpu.make_async_remote_copy(
+            src_ref=snd.at[c, pl.ds(0, 3)], dst_ref=kall.at[c, pl.ds(0, 3)],
+            send_sem=send_c.at[0], recv_sem=recv_c.at[c],
+            device_id={"tp": partner}, device_id_type=MESH).wait_recv()
 
     def repack(c):
         spread[...] = raw[c].reshape(B * BLK * 8, 64).astype(F32)
@@ -165,24 +147,21 @@
             spread[pl.ds(1, B * BLK, stride=2), :] = x[:, 64:]
             outs[c][:, pl.ds(s * 2 * BLK, 2 * BLK), :] = spread[pl.ds(0, 2 * B * BLK), :].astype(BF16).reshape(B, 2 * BLK, 64)
 
-    def x_desc(step, piece, n, slot):
-        sl = pl.ds(*PIECES[step % 2][piece])
-        return pltpu.make_async_remote_copy(
-            src_ref=xown.at[step, :, sl], dst_ref=xrecv.at[step, slot, :, sl],
-            send_sem=send_x.at[step, piece, n], recv_sem=recv_x.at[step, slot, piece],
-            device_id={"tp": peers[n]}, device_id_type=MESH)
-
     def x_send(step, piece, val):
         sl = pl.ds(*PIECES[step % 2][piece])
         xown[step, :, sl] = val
         for n in range(3):
-            x_desc(step, piece, n, me).start()
-            pending["xs", step, piece, n] = x_desc(step, piece, n, me).wait_send
-            pending["xr", step, piece, n] = x_desc(step, piece, n, peers[n]).wait_recv
+            pltpu.make_async_remote_copy(
+                src_ref=xown.at[step, :, sl], dst_ref=xrecv.at[step, me, :, sl],
+                send_sem=send_x.at[0], recv_sem=recv_x.at[step],
+                device_id={"tp": peers[n]}, device_id_type=MESH).start()
         xrecv[step, me, :, sl] = val
 
     def x_sum(step):
-        finish("xr", step)
+        pltpu.make_async_remote_copy(
+            src_ref=xrecv.at[step, pl.ds(0, 3)], dst_ref=xrecv.at[step, pl.ds(0, 3)],
+            send_sem=send_x.at[0], recv_sem=recv_x.at[step],
+            device_id={"tp": partner}, device_id_type=MESH).wait_recv()
         tot = xrecv[step, 0].astype(F32)
         for s in range(1, NTP):
             tot = tot + xrecv[step, s].astype(F32)
@@ -204,7 +183,7 @@
             jnp.where(left, q0, zero), jnp.where(left, pltpu.roll(q0, 64, 1), zero),
             jnp.where(left, zero, pltpu.roll(q1, 64, 1)), jnp.where(left, zero, q1)], axis=0).astype(BF16)
         kc, vc = 2 * l, 2 * l + 1
-        finish("cr", kc)
+        cache_wait(kc)
         k2d = kall[kc].reshape(NTP * B * BLK, 128)
         sc = lax.dot_general(qrows, k2d, (((1,), (1,)), ((), ())), preferred_element_type=F32) * 0.125
         sc = jnp.where(valid, sc, -1e30)
@@ -214,7 +193,7 @@
         den = jnp.sum(ex, axis=1, keepdims=True) + nex
         prob = (ex / den).astype(BF16)
         nprob = (nex / den).astype(BF16).astype(F32)
-        finish("cr", vc)
+        cache_wait(vc)
         v2d = kall[vc].reshape(NTP * B * BLK, 128)
         ov = jnp.dot(prob, v2d, preferred_element_type=F32) + nprob * jnp.concatenate([vnew] * 4, axis=0)
         attn = jnp.concatenate([jnp.where(left, ov[0:16], ov[48:64]), jnp.where(left, ov[16:32], ov[32:48])], axis=1).astype(BF16)
@@ -226,8 +205,8 @@
             cache_send(3, 1)
         emit(kc, knew)
         emit(vc, vnew)
-        for kind in "gud":
-            finish(kind, l)
+        for k in range(3):
+            w_copy(l, k).wait()
         if l == 0:
             start_layer(1)
         h1 = (h_f + x_sum(2 * l)).astype(BF16).astype(F32)
@@ -262,7 +241,12 @@
         h_f = (h1 + x_sum(2 * l + 1)).astype(BF16).astype(F32)
 
     hout[...] = h_f.astype(BF16)
-    finish()
+    pltpu.make_async_remote_copy(
+        src_ref=snd.at[:, pl.ds(0, 3)], dst_ref=kall.at[:, pl.ds(0, 3)], send_sem=send_c.at[0], recv_sem=recv_c.at[0],
+        device_id={"tp": partner}, device_id_type=MESH).wait_send()
+    pltpu.make_async_remote_copy(
+        src_ref=xrecv.at[:, pl.ds(0, 3)], dst_ref=xrecv.at[:, pl.ds(0, 3)], send_sem=send_x.at[0], recv_sem=recv_x.at[0],
+        device_id={"tp": partner}, device_id_type=MESH).wait_send()
 
 
 def _store(h, k1, v1, k2, v2, ho, ok1, ov1, ok2, ov2, sem):
@@ -300,8 +284,7 @@
                 V((1, 128), F32),
                 V((B * BLK * 8, 64), F32), V((4, NTP, B, BLK, 128), BF16), V((4, NTP, B, BLK, 128), BF16),
                 V((4, B, D), BF16), V((4, NTP, B, D), BF16), V((B, EXP * FL), BF16),
-                DMA((12,)), DMA((4,)), DMA((2, EXP // GCH)), DMA((2, EXP // GCH)), DMA((2, EXP // DCH)),
-                DMA((4, 3)), DMA((4, NTP)), DMA((4, NP, 3)), DMA((4, NTP, NP)),
+                DMA((11,)), DMA((4,)), DMA((2, 3)), DMA((1,)), DMA((4,)), DMA((1,)), DMA((4,)),
             ],
             compiler_params=pltpu.CompilerParams(collective_id=0, has_side_effects=True, vmem_limit_bytes=64_000_000),
         )(hidden, lengths.reshape(1, B), jnp.transpose(choice, (0, 2, 1)), keys_one, vals_one, keys_two, vals_two,

time: 35.5 us -> 34.5 us (0.972)
  Pallas kernels: 34.7 us -> 33.7 us
    pallas_call x1, Pallas kernels: 33.4 us -> 32.3 us  [local_step(): pl.pallas_call(_kernel, out_shape=tuple((V(s.shape, s.dtype) for s in sha...]
where the time goes in v9:
time: 34.5 us; the launch traced here: 34.3 us
  Pallas kernels  33.7 us (98%)
  between operations  0.65 us (2%)
    pallas_call x1, Pallas kernels, local_step(): pl.pallas_call(_kernel, out_shape=tuple((V(s.shape, s.dtype) for s in sha...  32.3 us
    pallas_call x1, Pallas kernels, local_step(): pl.pallas_call(_store, out_shape=shapes, in_specs=[vmem_spec] * 5, out_sp...  1.36 us

profile of v9, /device:TPU:0, one launch (start us, length us, event | category | flops | bytes accessed | tf_op | source)
XLA Modules:
  0.0 34.3 jit_solution(3022983294227065794)
XLA Ops:
  0.6 32.3 %shard_map.209 = (bf16[16,1024]{1,0:T(8,128)(2,1)S(1)}, bf16[16,128,64]{2,1,0:T(8,128)(2,1)S(1)}, bf16[16,128,64]{2,1,0:T(8,128)(2,1)S(1)}, bf16[16,128,64]{2,1,0:T(8,128)(2,1)S(1)}, bf16[16,128,64]{2,1,0:T(8,128)(2,1)S(1)}) custom-call(bf16[16,1024]{1,0:T(8,128)(2,1)} %hid_h.1, s32[1,16]{1,0:T(1,128)} %bitcast.9, s32[2,8,16]{2,1,0:T(8,128)} %bitcast.8, ...), custom_call_target="tpu_custom_call" | custom-call | tf_op jit(solution)/shard_map/pallas_call | solution.py:275
  33.0 1.4 %shard_map.210 = (bf16[16,1024]{1,0:T(8,128)(2,1)}, bf16[16,128,64]{2,1,0:T(8,128)(2,1)}, bf16[16,128,64]{2,1,0:T(8,128)(2,1)}, bf16[16,128,64]{2,1,0:T(8,128)(2,1)}, bf16[16,128,64]{2,1,0:T(8,128)(2,1)}) custom-call(bf16[16,1024]{1,0:T(8,128)(2,1)S(1)} %get-tuple-element.15.h, bf16[16,128,64]{2,1,0:T(8,128)(2,1)S(1)} %get-tuple-element.16.k1, ...), custom_call_target="tpu_custom_call" | custom-call | tf_op jit(solution)/shard_map/pallas_call | solution.py:292

commit v10 on v9

--- a/solution.py
+++ b/solution.py
@@ -19,8 +19,6 @@
 NTP = 4
 EXP = 32
 FL = 128
-GCH = 4
-DCH = 8
 PIECES = (((0, 1024),), ((0, 512), (512, 512)))
 NP = 2
 F32 = jnp.float32
@@ -40,8 +38,8 @@
 def _kernel(hid_h, len_h, cho_h, k1_h, v1_h, k2_h, v2_h, ga_h, wq_h, wk_h, wv_h, wo_h, gm_h, wr_h, wg_h, wu_h, wd_h, inv_h,
             hout, ok1, ov1, ok2, ov2,
             hid, lens, cho, raw, ga, wq, wk, wv, wo, gm, wr, wg, wu, wd, inv,
-            spread, snd, kall, xown, xrecv, act,
-            sem_s, sem_raw, sem_w, send_c, recv_c, send_x, recv_x):
+            spread, snd, kall, xown, xrecv, act, qown, qx, sown, sx, emat,
+            sem_s, sem_raw, sem_w, send_c, recv_c, send_x, recv_x, send_q, recv_q, send_s, recv_s):
     me = lax.axis_index("tp")
     chip, core = me // 2, me % 2
     partner = chip * 2 + (1 - core)
@@ -68,8 +66,11 @@
         src, dst = ((wg_h, wg), (wu_h, wu), (wd_h, wd))[k]
         return pltpu.make_async_copy(src.at[l], dst.at[l], sem_w.at[l, k])
 
+    FIRST = (0, 1, 3, 5, 6, 7, 8)
+    for i in FIRST:
+        small_copy(i).start()
+    raw_copy(1).start()
     raw_copy(0).start()
-    raw_copy(1).start()
 
     def start_layer(l):
         for k in range(3):
@@ -95,30 +96,8 @@
             snd[c, p] = jnp.concatenate([lo, hi], axis=1).astype(BF16).reshape(B, BLK, 128)
         kall[c, me] = snd[c, me]
 
-    raw_copy(0).wait()
-    for i in range(len(smalls)):
-        small_copy(i).start()
-    repack(0)
-    pl.semaphore_wait(barrier, 3)
-    for n in range(3):
-        cache_send(0, n)
-    raw_copy(1).wait()
-    raw_copy(2).start()
-    raw_copy(3).start()
-    repack(1)
-    for n in range(3):
-        cache_send(1, n)
-    for i in range(len(smalls)):
+    for i in FIRST:
         small_copy(i).wait()
-    raw_copy(2).wait()
-    raw_copy(3).wait()
-    start_layer(0)
-    repack(2)
-    cache_send(2, 0)
-    cache_send(2, 2)
-    repack(3)
-    cache_send(3, 2)
-
 
     eye = lax.broadcasted_iota(jnp.int32, (B, B), 0) == lax.broadcasted_iota(jnp.int32, (B, B), 1)
     len_row = jnp.broadcast_to(lens[...].astype(F32), (B, B))
@@ -137,6 +116,80 @@
 
     h_f = hid[...].astype(F32)
 
+    def project(l, h_f):
+        a = _norm(h_f, ga[pl.ds(l, 1), :].astype(F32))
+        qf = jnp.dot(a, wq[l], preferred_element_type=F32)
+        kf = jnp.dot(a, wk[l], preferred_element_type=F32)
+        vf = jnp.dot(a, wv[l], preferred_element_type=F32)
+        q = jnp.concatenate([_rope(qf[:, :128], cosv, sinv, low), _rope(qf[:, 128:], cosv, sinv, low)], axis=1).astype(BF16)
+        return q, _rope(kf, cosv, sinv, low).astype(BF16).astype(F32), vf.astype(BF16).astype(F32)
+
+    def head_rows(q):
+        q0, q1 = q[:, :128].astype(F32), q[:, 128:].astype(F32)
+        zero = jnp.zeros_like(q0)
+        return jnp.concatenate([
+            jnp.where(left, q0, zero), jnp.where(left, pltpu.roll(q0, 64, 1), zero),
+            jnp.where(left, zero, pltpu.roll(q1, 64, 1)), jnp.where(left, zero, q1)], axis=0).astype(BF16)
+
+    def swap(src, dst, send, recv, n):
+        pltpu.make_async_remote_copy(src_ref=src, dst_ref=dst, send_sem=send.at[0], recv_sem=recv.at[0],
+                                     device_id={"tp": peers[n]}, device_id_type=MESH).start()
+
+    def swapped(ref, send, recv):
+        return pltpu.make_async_remote_copy(src_ref=ref.at[pl.ds(0, 3)], dst_ref=ref.at[pl.ds(0, 3)], send_sem=send.at[0],
+                                            recv_sem=recv.at[0], device_id={"tp": partner}, device_id_type=MESH)
+
+    q, knew, vnew = project(0, h_f)
+    qown[...] = q
+    pl.semaphore_wait(barrier, 3)
+    for n in range(3):
+        swap(qown, qx.at[me], send_q, recv_q, n)
+    qx[me] = q
+    raw_copy(1).wait()
+    repack(1)
+    for n in range(3):
+        cache_send(1, n)
+    raw_copy(0).wait()
+    for i in range(len(smalls)):
+        if i not in FIRST:
+            small_copy(i).start()
+    raw_copy(2).start()
+    raw_copy(3).start()
+    repack(0)
+    lane8 = lax.broadcasted_iota(jnp.int32, (8, 128), 1) // BLK
+    colk = lax.broadcasted_iota(jnp.int32, (64, 256), 1)
+    rowk = lax.broadcasted_iota(jnp.int32, (64, 256), 0)
+    own_b = ((colk // BLK) % B) == (rowk % B)
+    ecol = lax.broadcasted_iota(jnp.int32, (128, 1024), 1)
+    erow = lax.broadcasted_iota(jnp.int32, (128, 1024), 0)
+    emat[...] = jnp.where((ecol // 256) * BLK + ecol % BLK == erow, 1.0, 0.0).astype(BF16)
+    swapped(qx, send_q, recv_q).wait_recv()
+    for p in range(NTP):
+        sk = lax.dot_general(head_rows(qx[p]), snd[0, p].reshape(B * BLK, 128), (((1,), (1,)), ((), ())), preferred_element_type=F32) * 0.125
+        sk = jnp.where(own_b, sk, 0.0)
+        sk = sk[:, :128] + sk[:, 128:]
+        for shift in (64, 32, 16):
+            sk = sk + pltpu.roll(sk, shift, 1)
+        packed = sk[0:8]
+        for k in range(1, 8):
+            packed = jnp.where(lane8 == k, sk[8 * k:8 * k + 8], packed)
+        sown[p] = packed
+    for n in range(3):
+        swap(sown.at[peers[n]], sx.at[me], send_s, recv_s, n)
+    sx[me] = sown[me]
+    for i in range(len(smalls)):
+        if i not in FIRST:
+            small_copy(i).wait()
+    raw_copy(2).wait()
+    raw_copy(3).wait()
+    start_layer(0)
+    repack(2)
+    cache_send(2, 0)
+    cache_send(2, 2)
+    repack(3)
+    cache_send(3, 2)
+    cache_send(0, 2)
+
     def emit(c, new):
         new3 = jnp.broadcast_to(new[:, None, :], (B, BLK, 128))
         len3 = jnp.broadcast_to(len_b[:, None, :], (B, BLK, 128))
@@ -170,29 +223,37 @@
     outs = (ok1, ov1, ok2, ov2)
 
     for l in range(2):
-        a = _norm(h_f, ga[pl.ds(l, 1), :].astype(F32))
-        qf = jnp.dot(a, wq[l], preferred_element_type=F32)
-        kf = jnp.dot(a, wk[l], preferred_element_type=F32)
-        vf = jnp.dot(a, wv[l], preferred_element_type=F32)
-        q0 = _rope(qf[:, :128], cosv, sinv, low)
-        q1 = _rope(qf[:, 128:], cosv, sinv, low)
-        knew = _rope(kf, cosv, sinv, low).astype(BF16).astype(F32)
-        vnew = vf.astype(BF16).astype(F32)
-        zero = jnp.zeros_like(q0)
-        qrows = jnp.concatenate([
-            jnp.where(left, q0, zero), jnp.where(left, pltpu.roll(q0, 64, 1), zero),
-            jnp.where(left, zero, pltpu.roll(q1, 64, 1)), jnp.where(left, zero, q1)], axis=0).astype(BF16)
+        if l == 1:
+            q, knew, vnew = project(l, h_f)
+        qrows = head_rows(q)
         kc, vc = 2 * l, 2 * l + 1
-        cache_wait(kc)
-        k2d = kall[kc].reshape(NTP * B * BLK, 128)
-        sc = lax.dot_general(qrows, k2d, (((1,), (1,)), ((), ())), preferred_element_type=F32) * 0.125
-        sc = jnp.where(valid, sc, -1e30)
         ns = jnp.sum(qrows.astype(F32) * jnp.concatenate([knew] * 4, axis=0), axis=1, keepdims=True) * 0.125
+        if l == 0:
+            swapped(sx, send_s, recv_s).wait_recv()
+            rows = []
+            for k in range(8):
+                acc = jnp.zeros((8, 128), F32)
+                for sd in range(NTP):
+                    shift = (BLK * (sd - k)) % 128
+                    part = sx[sd] if shift == 0 else pltpu.roll(sx[sd], shift, 1)
+                    acc = jnp.where(lane8 == sd, part, acc)
+                rows.append(acc)
+            sc = jnp.concatenate(rows, axis=0)
+            ok = lax.broadcasted_iota(jnp.int32, (64, 128), 1).astype(F32) < len64
+        else:
+            cache_wait(kc)
+            k2d = kall[kc].reshape(NTP * B * BLK, 128)
+            sc = lax.dot_general(qrows, k2d, (((1,), (1,)), ((), ())), preferred_element_type=F32) * 0.125
+            ok = valid
+        sc = jnp.where(ok, sc, -1e30)
         top = jnp.maximum(jnp.max(sc, axis=1, keepdims=True), ns)
         ex, nex = jnp.exp(sc - top), jnp.exp(ns - top)
         den = jnp.sum(ex, axis=1, keepdims=True) + nex
         prob = (ex / den).astype(BF16)
         nprob = (nex / den).astype(BF16).astype(F32)
+        if l == 0:
+            wide = jnp.dot(prob, emat[...], preferred_element_type=F32)
+            prob = jnp.where(valid, wide, 0.0).astype(BF16)
         cache_wait(vc)
         v2d = kall[vc].reshape(NTP * B * BLK, 128)
         ov = jnp.dot(prob, v2d, preferred_element_type=F32) + nprob * jnp.concatenate([vnew] * 4, axis=0)
@@ -203,7 +264,10 @@
             cache_send(2, 1)
             cache_send(3, 0)
             cache_send(3, 1)
-        emit(kc, knew)
+        else:
+            cache_send(0, 0)
+            cache_send(0, 1)
+            emit(kc, knew)
         emit(vc, vnew)
         for k in range(3):
             w_copy(l, k).wait()
@@ -238,9 +302,16 @@
         x_send(2 * l + 1, 0, acc0.astype(BF16))
         acc1 = down(1, range(8, EXP, 2), acc1)
         x_send(2 * l + 1, 1, acc1.astype(BF16))
+        if l == 0:
+            kone = knew
+        else:
+            cache_wait(0)
+            emit(0, kone)
         h_f = (h1 + x_sum(2 * l + 1)).astype(BF16).astype(F32)
 
     hout[...] = h_f.astype(BF16)
+    swapped(qx, send_q, recv_q).wait_send()
+    swapped(sx, send_s, recv_s).wait_send()
     pltpu.make_async_remote_copy(
         src_ref=snd.at[:, pl.ds(0, 3)], dst_ref=kall.at[:, pl.ds(0, 3)], send_sem=send_c.at[0], recv_sem=recv_c.at[0],
         device_id={"tp": partner}, device_id_type=MESH).wait_send()
@@ -283,8 +354,8 @@
                 V((2, D), BF16), V((2, EXP, D), BF16), V((2, EXP, D, FL), BF16), V((2, EXP, D, FL), BF16), V((2, EXP, FL, D), BF16),
                 V((1, 128), F32),
                 V((B * BLK * 8, 64), F32), V((4, NTP, B, BLK, 128), BF16), V((4, NTP, B, BLK, 128), BF16),
-                V((4, B, D), BF16), V((4, NTP, B, D), BF16), V((B, EXP * FL), BF16),
-                DMA((11,)), DMA((4,)), DMA((2, 3)), DMA((1,)), DMA((4,)), DMA((1,)), DMA((4,)),
+                V((4, B, D), BF16), V((4, NTP, B, D), BF16), V((B, EXP * FL), BF16), V((B, 256), BF16), V((NTP, B, 256), BF16), V((NTP, 8, 128), F32), V((NTP, 8, 128), F32), V((128, 1024), BF16),
+                DMA((11,)), DMA((4,)), DMA((2, 3)), DMA((1,)), DMA((4,)), DMA((1,)), DMA((4,)), DMA((1,)), DMA((1,)), DMA((1,)), DMA((1,)),
             ],
             compiler_params=pltpu.CompilerParams(collective_id=0, has_side_effects=True, vmem_limit_bytes=64_000_000),
         )(hidden, lengths.reshape(1, B), jnp.transpose(choice, (0, 2, 1)), keys_one, vals_one, keys_two, vals_two,

time: 34.5 us -> 34.7 us (level)
  no operation moved by 1% of the time
where the time goes in v10:
time: 34.7 us; the launch traced here: 34.6 us
  Pallas kernels  34 us (98%)
  between operations  0.65 us (2%)
    pallas_call x1, Pallas kernels, local_step(): pl.pallas_call(_kernel, out_shape=tuple((V(s.shape, s.dtype) for s in sha...  32.6 us
    pallas_call x1, Pallas kernels, local_step(): pl.pallas_call(_store, out_shape=shapes, in_specs=[vmem_spec] * 5, out_sp...  1.36 us

profile of v10, /device:TPU:0, one launch (start us, length us, event | category | flops | bytes accessed | tf_op | source)
XLA Modules:
  0.0 34.6 jit_solution(9843833382967166285)
XLA Ops:
  0.6 32.6 %shard_map.209 = (bf16[16,1024]{1,0:T(8,128)(2,1)S(1)}, bf16[16,128,64]{2,1,0:T(8,128)(2,1)S(1)}, bf16[16,128,64]{2,1,0:T(8,128)(2,1)S(1)}, bf16[16,128,64]{2,1,0:T(8,128)(2,1)S(1)}, bf16[16,128,64]{2,1,0:T(8,128)(2,1)S(1)}) custom-call(bf16[16,1024]{1,0:T(8,128)(2,1)} %hid_h.1, s32[1,16]{1,0:T(1,128)} %bitcast.9, s32[2,8,16]{2,1,0:T(8,128)} %bitcast.8, ...), custom_call_target="tpu_custom_call" | custom-call | tf_op jit(solution)/shard_map/pallas_call | solution.py:346
  33.3 1.4 %shard_map.210 = (bf16[16,1024]{1,0:T(8,128)(2,1)}, bf16[16,128,64]{2,1,0:T(8,128)(2,1)}, bf16[16,128,64]{2,1,0:T(8,128)(2,1)}, bf16[16,128,64]{2,1,0:T(8,128)(2,1)}, bf16[16,128,64]{2,1,0:T(8,128)(2,1)}) custom-call(bf16[16,1024]{1,0:T(8,128)(2,1)S(1)} %get-tuple-element.15.h, bf16[16,128,64]{2,1,0:T(8,128)(2,1)S(1)} %get-tuple-element.16.k1, ...), custom_call_target="tpu_custom_call" | custom-call | tf_op jit(solution)/shard_map/pallas_call | solution.py:363

commit v11 on v10

--- a/solution.py
+++ b/solution.py
@@ -73,8 +73,11 @@
     raw_copy(0).start()
 
     def start_layer(l):
-        for k in range(3):
-            w_copy(l, k).start()
+        for i in range(0, EXP, 4):
+            for k in range(3):
+                src, dst = ((wg_h, wg), (wu_h, wu), (wd_h, wd))[k]
+                sl = pl.ds(i, 4)
+                pltpu.make_async_copy(src.at[l, sl], dst.at[l, sl], sem_w.at[l, k]).start()
 
     def cache_send(c, n):
         pltpu.make_async_remote_copy(
@@ -155,6 +158,7 @@
             small_copy(i).start()
     raw_copy(2).start()
     raw_copy(3).start()
+    start_layer(0)
     repack(0)
     lane8 = lax.broadcasted_iota(jnp.int32, (8, 128), 1) // BLK
     colk = lax.broadcasted_iota(jnp.int32, (64, 256), 1)
@@ -182,7 +186,6 @@
             small_copy(i).wait()
     raw_copy(2).wait()
     raw_copy(3).wait()
-    start_layer(0)
     repack(2)
     cache_send(2, 0)
     cache_send(2, 2)

time: 34.7 us -> 37.6 us (1.084)
  Pallas kernels: 34 us -> 36.9 us
    pallas_call x1, Pallas kernels: 32.6 us -> 35.5 us  [local_step(): pl.pallas_call(_kernel, out_shape=tuple((V(s.shape, s.dtype) for s in sha...]
where the time goes in v11:
time: 37.6 us; the launch traced here: 37.5 us
  Pallas kernels  36.9 us (98%)
  between operations  0.65 us (2%)
    pallas_call x1, Pallas kernels, local_step(): pl.pallas_call(_kernel, out_shape=tuple((V(s.shape, s.dtype) for s in sha...  35.5 us
    pallas_call x1, Pallas kernels, local_step(): pl.pallas_call(_store, out_shape=shapes, in_specs=[vmem_spec] * 5, out_sp...  1.36 us

profile of v11, /device:TPU:0, one launch (start us, length us, event | category | flops | bytes accessed | tf_op | source)
XLA Modules:
  0.0 37.5 jit_solution(6358123709269101383)
XLA Ops:
  0.6 35.5 %shard_map.209 = (bf16[16,1024]{1,0:T(8,128)(2,1)S(1)}, bf16[16,128,64]{2,1,0:T(8,128)(2,1)S(1)}, bf16[16,128,64]{2,1,0:T(8,128)(2,1)S(1)}, bf16[16,128,64]{2,1,0:T(8,128)(2,1)S(1)}, bf16[16,128,64]{2,1,0:T(8,128)(2,1)S(1)}) custom-call(bf16[16,1024]{1,0:T(8,128)(2,1)} %hid_h.1, s32[1,16]{1,0:T(1,128)} %bitcast.9, s32[2,8,16]{2,1,0:T(8,128)} %bitcast.8, ...), custom_call_target="tpu_custom_call" | custom-call | tf_op jit(solution)/shard_map/pallas_call | solution.py:349
  36.1 1.4 %shard_map.210 = (bf16[16,1024]{1,0:T(8,128)(2,1)}, bf16[16,128,64]{2,1,0:T(8,128)(2,1)}, bf16[16,128,64]{2,1,0:T(8,128)(2,1)}, bf16[16,128,64]{2,1,0:T(8,128)(2,1)}, bf16[16,128,64]{2,1,0:T(8,128)(2,1)}) custom-call(bf16[16,1024]{1,0:T(8,128)(2,1)S(1)} %get-tuple-element.15.h, bf16[16,128,64]{2,1,0:T(8,128)(2,1)S(1)} %get-tuple-element.16.k1, ...), custom_call_target="tpu_custom_call" | custom-call | tf_op jit(solution)/shard_map/pallas_call | solution.py:366

commit v12 on v10

--- a/solution.py
+++ b/solution.py
@@ -57,7 +57,8 @@
         return pltpu.make_async_copy(raw_src[c], raw.at[c], sem_raw.at[c])
 
     smalls = ((hid_h, hid), (len_h, lens), (cho_h, cho), (ga_h, ga), (gm_h, gm), (inv_h, inv),
-              (wq_h, wq), (wk_h, wk), (wv_h, wv), (wo_h, wo), (wr_h, wr))
+              (wq_h.at[0], wq.at[0]), (wk_h.at[0], wk.at[0]), (wv_h.at[0], wv.at[0]), (wo_h, wo), (wr_h, wr),
+              (wq_h.at[1], wq.at[1]), (wk_h.at[1], wk.at[1]), (wv_h.at[1], wv.at[1]))
 
     def small_copy(i):
         return pltpu.make_async_copy(smalls[i][0], smalls[i][1], sem_s.at[i])
@@ -70,7 +71,6 @@
     for i in FIRST:
         small_copy(i).start()
     raw_copy(1).start()
-    raw_copy(0).start()
 
     def start_layer(l):
         for k in range(3):
@@ -98,6 +98,12 @@
 
     for i in FIRST:
         small_copy(i).wait()
+    raw_copy(0).start()
+    for i in (2, 4, 9, 10):
+        small_copy(i).start()
+    raw_copy(2).start()
+    raw_copy(3).start()
+    w_copy(0, 0).start()
 
     eye = lax.broadcasted_iota(jnp.int32, (B, B), 0) == lax.broadcasted_iota(jnp.int32, (B, B), 1)
     len_row = jnp.broadcast_to(lens[...].astype(F32), (B, B))
@@ -150,11 +156,6 @@
     for n in range(3):
         cache_send(1, n)
     raw_copy(0).wait()
-    for i in range(len(smalls)):
-        if i not in FIRST:
-            small_copy(i).start()
-    raw_copy(2).start()
-    raw_copy(3).start()
     repack(0)
     lane8 = lax.broadcasted_iota(jnp.int32, (8, 128), 1) // BLK
     colk = lax.broadcasted_iota(jnp.int32, (64, 256), 1)
@@ -163,6 +164,14 @@
     ecol = lax.broadcasted_iota(jnp.int32, (128, 1024), 1)
     erow = lax.broadcasted_iota(jnp.int32, (128, 1024), 0)
     emat[...] = jnp.where((ecol // 256) * BLK + ecol % BLK == erow, 1.0, 0.0).astype(BF16)
+    for i in (2, 4, 9, 10):
+        small_copy(i).wait()
+    raw_copy(2).wait()
+    raw_copy(3).wait()
+    w_copy(0, 1).start()
+    w_copy(0, 2).start()
+    for i in (11, 12, 13):
+        small_copy(i).start()
     swapped(qx, send_q, recv_q).wait_recv()
     for p in range(NTP):
         sk = lax.dot_general(head_rows(qx[p]), snd[0, p].reshape(B * BLK, 128), (((1,), (1,)), ((), ())), preferred_element_type=F32) * 0.125
@@ -177,12 +186,6 @@
     for n in range(3):
         swap(sown.at[peers[n]], sx.at[me], send_s, recv_s, n)
     sx[me] = sown[me]
-    for i in range(len(smalls)):
-        if i not in FIRST:
-            small_copy(i).wait()
-    raw_copy(2).wait()
-    raw_copy(3).wait()
-    start_layer(0)
     repack(2)
     cache_send(2, 0)
     cache_send(2, 2)
@@ -273,6 +276,8 @@
             w_copy(l, k).wait()
         if l == 0:
             start_layer(1)
+            for i in (11, 12, 13):
+                small_copy(i).wait()
         h1 = (h_f + x_sum(2 * l)).astype(BF16).astype(F32)
         m = _norm(h1, gm[pl.ds(l, 1), :].astype(F32))
 
@@ -355,7 +360,7 @@
                 V((1, 128), F32),
                 V((B * BLK * 8, 64), F32), V((4, NTP, B, BLK, 128), BF16), V((4, NTP, B, BLK, 128), BF16),
                 V((4, B, D), BF16), V((4, NTP, B, D), BF16), V((B, EXP * FL), BF16), V((B, 256), BF16), V((NTP, B, 256), BF16), V((NTP, 8, 128), F32), V((NTP, 8, 128), F32), V((128, 1024), BF16),
-                DMA((11,)), DMA((4,)), DMA((2, 3)), DMA((1,)), DMA((4,)), DMA((1,)), DMA((4,)), DMA((1,)), DMA((1,)), DMA((1,)), DMA((1,)),
+                DMA((14,)), DMA((4,)), DMA((2, 3)), DMA((1,)), DMA((4,)), DMA((1,)), DMA((4,)), DMA((1,)), DMA((1,)), DMA((1,)), DMA((1,)),
             ],
             compiler_params=pltpu.CompilerParams(collective_id=0, has_side_effects=True, vmem_limit_bytes=64_000_000),
         )(hidden, lengths.reshape(1, B), jnp.transpose(choice, (0, 2, 1)), keys_one, vals_one, keys_two, vals_two,

time: 34.7 us -> 35.5 us (1.023)
  Pallas kernels: 34 us -> 34.7 us
    pallas_call x1, Pallas kernels: 32.6 us -> 33.3 us  [local_step(): pl.pallas_call(_kernel, out_shape=tuple((V(s.shape, s.dtype) for s in sha...]
where the time goes in v12:
time: 35.5 us; the launch traced here: 35.4 us
  Pallas kernels  34.7 us (98%)
  between operations  0.65 us (2%)
    pallas_call x1, Pallas kernels, local_step(): pl.pallas_call(_kernel, out_shape=tuple((V(s.shape, s.dtype) for s in sha...  33.3 us
    pallas_call x1, Pallas kernels, local_step(): pl.pallas_call(_store, out_shape=shapes, in_specs=[vmem_spec] * 5, out_sp...  1.36 us

profile of v12, /device:TPU:0, one launch (start us, length us, event | category | flops | bytes accessed | tf_op | source)
XLA Modules:
  0.0 35.4 jit_solution(13573272964628269980)
XLA Ops:
  0.6 33.3 %shard_map.209 = (bf16[16,1024]{1,0:T(8,128)(2,1)S(1)}, bf16[16,128,64]{2,1,0:T(8,128)(2,1)S(1)}, bf16[16,128,64]{2,1,0:T(8,128)(2,1)S(1)}, bf16[16,128,64]{2,1,0:T(8,128)(2,1)S(1)}, bf16[16,128,64]{2,1,0:T(8,128)(2,1)S(1)}) custom-call(bf16[16,1024]{1,0:T(8,128)(2,1)} %hid_h.1, s32[1,16]{1,0:T(1,128)} %bitcast.9, s32[2,8,16]{2,1,0:T(8,128)} %bitcast.8, ...), custom_call_target="tpu_custom_call" | custom-call | tf_op jit(solution)/shard_map/pallas_call | solution.py:351
  34.0 1.4 %shard_map.210 = (bf16[16,1024]{1,0:T(8,128)(2,1)}, bf16[16,128,64]{2,1,0:T(8,128)(2,1)}, bf16[16,128,64]{2,1,0:T(8,128)(2,1)}, bf16[16,128,64]{2,1,0:T(8,128)(2,1)}, bf16[16,128,64]{2,1,0:T(8,128)(2,1)}) custom-call(bf16[16,1024]{1,0:T(8,128)(2,1)S(1)} %get-tuple-element.15.h, bf16[16,128,64]{2,1,0:T(8,128)(2,1)S(1)} %get-tuple-element.16.k1, ...), custom_call_target="tpu_custom_call" | custom-call | tf_op jit(solution)/shard_map/pallas_call | solution.py:368

commit v13 on v9

--- a/solution.py
+++ b/solution.py
@@ -19,8 +19,6 @@
 NTP = 4
 EXP = 32
 FL = 128
-GCH = 4
-DCH = 8
 PIECES = (((0, 1024),), ((0, 512), (512, 512)))
 NP = 2
 F32 = jnp.float32
@@ -70,10 +68,6 @@
 
     raw_copy(0).start()
     raw_copy(1).start()
-
-    def start_layer(l):
-        for k in range(3):
-            w_copy(l, k).start()
 
     def cache_send(c, n):
         pltpu.make_async_remote_copy(
@@ -112,7 +106,8 @@
         small_copy(i).wait()
     raw_copy(2).wait()
     raw_copy(3).wait()
-    start_layer(0)
+    w_copy(0, 0).start()
+    w_copy(0, 1).start()
     repack(2)
     cache_send(2, 0)
     cache_send(2, 2)
@@ -183,6 +178,10 @@
             jnp.where(left, q0, zero), jnp.where(left, pltpu.roll(q0, 64, 1), zero),
             jnp.where(left, zero, pltpu.roll(q1, 64, 1)), jnp.where(left, zero, q1)], axis=0).astype(BF16)
         kc, vc = 2 * l, 2 * l + 1
+        if l == 0:
+            w_copy(0, 0).wait()
+            w_copy(0, 1).wait()
+            w_copy(0, 2).start()
         cache_wait(kc)
         k2d = kall[kc].reshape(NTP * B * BLK, 128)
         sc = lax.dot_general(qrows, k2d, (((1,), (1,)), ((), ())), preferred_element_type=F32) * 0.125
@@ -200,15 +199,19 @@
         wo_rows = jnp.concatenate([wo[l, pl.ds(0, 64), :], wo[l, pl.ds(192, 64), :], wo[l, pl.ds(64, 128), :]], axis=0)
         x_send(2 * l, 0, jnp.dot(attn, wo_rows, preferred_element_type=F32).astype(BF16))
         if l == 0:
+            w_copy(1, 0).start()
             cache_send(2, 1)
             cache_send(3, 0)
             cache_send(3, 1)
         emit(kc, knew)
         emit(vc, vnew)
-        for k in range(3):
-            w_copy(l, k).wait()
         if l == 0:
-            start_layer(1)
+            w_copy(0, 2).wait()
+            w_copy(1, 1).start()
+            w_copy(1, 2).start()
+        else:
+            for k in range(3):
+                w_copy(1, k).wait()
         h1 = (h_f + x_sum(2 * l)).astype(BF16).astype(F32)
         m = _norm(h1, gm[pl.ds(l, 1), :].astype(F32))
 

time: 34.5 us -> 34.5 us (level)
  no operation moved by 1% of the time
where the time goes in v13:
time: 34.5 us; the launch traced here: 34.3 us
  Pallas kernels  33.7 us (98%)
  between operations  0.65 us (2%)
    pallas_call x1, Pallas kernels, local_step(): pl.pallas_call(_kernel, out_shape=tuple((V(s.shape, s.dtype) for s in sha...  32.3 us
    pallas_call x1, Pallas kernels, local_step(): pl.pallas_call(_store, out_shape=shapes, in_specs=[vmem_spec] * 5, out_sp...  1.36 us

profile of v13, /device:TPU:0, one launch (start us, length us, event | category | flops | bytes accessed | tf_op | source)
XLA Modules:
  0.0 34.3 jit_solution(15989674848874420203)
XLA Ops:
  0.6 32.3 %shard_map.209 = (bf16[16,1024]{1,0:T(8,128)(2,1)S(1)}, bf16[16,128,64]{2,1,0:T(8,128)(2,1)S(1)}, bf16[16,128,64]{2,1,0:T(8,128)(2,1)S(1)}, bf16[16,128,64]{2,1,0:T(8,128)(2,1)S(1)}, bf16[16,128,64]{2,1,0:T(8,128)(2,1)S(1)}) custom-call(bf16[16,1024]{1,0:T(8,128)(2,1)} %hid_h.1, s32[1,16]{1,0:T(1,128)} %bitcast.9, s32[2,8,16]{2,1,0:T(8,128)} %bitcast.8, ...), custom_call_target="tpu_custom_call" | custom-call | tf_op jit(solution)/shard_map/pallas_call | solution.py:278
  33.0 1.4 %shard_map.210 = (bf16[16,1024]{1,0:T(8,128)(2,1)}, bf16[16,128,64]{2,1,0:T(8,128)(2,1)}, bf16[16,128,64]{2,1,0:T(8,128)(2,1)}, bf16[16,128,64]{2,1,0:T(8,128)(2,1)}, bf16[16,128,64]{2,1,0:T(8,128)(2,1)}) custom-call(bf16[16,1024]{1,0:T(8,128)(2,1)S(1)} %get-tuple-element.15.h, bf16[16,128,64]{2,1,0:T(8,128)(2,1)S(1)} %get-tuple-element.16.k1, ...), custom_call_target="tpu_custom_call" | custom-call | tf_op jit(solution)/shard_map/pallas_call | solution.py:295

commit v14 on v10

--- a/solution.py
+++ b/solution.py
@@ -163,6 +163,12 @@
     ecol = lax.broadcasted_iota(jnp.int32, (128, 1024), 1)
     erow = lax.broadcasted_iota(jnp.int32, (128, 1024), 0)
     emat[...] = jnp.where((ecol // 256) * BLK + ecol % BLK == erow, 1.0, 0.0).astype(BF16)
+    for i in range(len(smalls)):
+        if i not in FIRST:
+            small_copy(i).wait()
+    raw_copy(2).wait()
+    raw_copy(3).wait()
+    start_layer(0)
     swapped(qx, send_q, recv_q).wait_recv()
     for p in range(NTP):
         sk = lax.dot_general(head_rows(qx[p]), snd[0, p].reshape(B * BLK, 128), (((1,), (1,)), ((), ())), preferred_element_type=F32) * 0.125
@@ -177,12 +183,6 @@
     for n in range(3):
         swap(sown.at[peers[n]], sx.at[me], send_s, recv_s, n)
     sx[me] = sown[me]
-    for i in range(len(smalls)):
-        if i not in FIRST:
-            small_copy(i).wait()
-    raw_copy(2).wait()
-    raw_copy(3).wait()
-    start_layer(0)
     repack(2)
     cache_send(2, 0)
     cache_send(2, 2)

time: 34.7 us -> 34.6 us (level)
  no operation moved by 1% of the time
where the time goes in v14:
time: 34.6 us; the launch traced here: 34.5 us
  Pallas kernels  33.8 us (98%)
  between operations  0.65 us (2%)
    pallas_call x1, Pallas kernels, local_step(): pl.pallas_call(_kernel, out_shape=tuple((V(s.shape, s.dtype) for s in sha...  32.5 us
    pallas_call x1, Pallas kernels, local_step(): pl.pallas_call(_store, out_shape=shapes, in_specs=[vmem_spec] * 5, out_sp...  1.36 us

profile of v14, /device:TPU:0, one launch (start us, length us, event | category | flops | bytes accessed | tf_op | source)
XLA Modules:
  0.0 34.5 jit_solution(11050296912987941451)
XLA Ops:
  0.6 32.5 %shard_map.209 = (bf16[16,1024]{1,0:T(8,128)(2,1)S(1)}, bf16[16,128,64]{2,1,0:T(8,128)(2,1)S(1)}, bf16[16,128,64]{2,1,0:T(8,128)(2,1)S(1)}, bf16[16,128,64]{2,1,0:T(8,128)(2,1)S(1)}, bf16[16,128,64]{2,1,0:T(8,128)(2,1)S(1)}) custom-call(bf16[16,1024]{1,0:T(8,128)(2,1)} %hid_h.1, s32[1,16]{1,0:T(1,128)} %bitcast.9, s32[2,8,16]{2,1,0:T(8,128)} %bitcast.8, ...), custom_call_target="tpu_custom_call" | custom-call | tf_op jit(solution)/shard_map/pallas_call | solution.py:346
  33.1 1.4 %shard_map.210 = (bf16[16,1024]{1,0:T(8,128)(2,1)}, bf16[16,128,64]{2,1,0:T(8,128)(2,1)}, bf16[16,128,64]{2,1,0:T(8,128)(2,1)}, bf16[16,128,64]{2,1,0:T(8,128)(2,1)}, bf16[16,128,64]{2,1,0:T(8,128)(2,1)}) custom-call(bf16[16,1024]{1,0:T(8,128)(2,1)S(1)} %get-tuple-element.15.h, bf16[16,128,64]{2,1,0:T(8,128)(2,1)S(1)} %get-tuple-element.16.k1, ...), custom_call_target="tpu_custom_call" | custom-call | tf_op jit(solution)/shard_map/pallas_call | solution.py:363

commit v15 on v14

--- a/solution.py
+++ b/solution.py
@@ -57,7 +57,8 @@
         return pltpu.make_async_copy(raw_src[c], raw.at[c], sem_raw.at[c])
 
     smalls = ((hid_h, hid), (len_h, lens), (cho_h, cho), (ga_h, ga), (gm_h, gm), (inv_h, inv),
-              (wq_h, wq), (wk_h, wk), (wv_h, wv), (wo_h, wo), (wr_h, wr))
+              (wq_h.at[0], wq.at[0]), (wk_h.at[0], wk.at[0]), (wv_h.at[0], wv.at[0]), (wo_h, wo), (wr_h, wr),
+              (wq_h.at[1], wq.at[1]), (wk_h.at[1], wk.at[1]), (wv_h.at[1], wv.at[1]))
 
     def small_copy(i):
         return pltpu.make_async_copy(smalls[i][0], smalls[i][1], sem_s.at[i])
@@ -70,7 +71,6 @@
     for i in FIRST:
         small_copy(i).start()
     raw_copy(1).start()
-    raw_copy(0).start()
 
     def start_layer(l):
         for k in range(3):
@@ -98,6 +98,12 @@
 
     for i in FIRST:
         small_copy(i).wait()
+    raw_copy(0).start()
+    for i in range(len(smalls)):
+        if i not in FIRST:
+            small_copy(i).start()
+    raw_copy(2).start()
+    raw_copy(3).start()
 
     eye = lax.broadcasted_iota(jnp.int32, (B, B), 0) == lax.broadcasted_iota(jnp.int32, (B, B), 1)
     len_row = jnp.broadcast_to(lens[...].astype(F32), (B, B))
@@ -150,11 +156,6 @@
     for n in range(3):
         cache_send(1, n)
     raw_copy(0).wait()
-    for i in range(len(smalls)):
-        if i not in FIRST:
-            small_copy(i).start()
-    raw_copy(2).start()
-    raw_copy(3).start()
     repack(0)
     lane8 = lax.broadcasted_iota(jnp.int32, (8, 128), 1) // BLK
     colk = lax.broadcasted_iota(jnp.int32, (64, 256), 1)
@@ -355,7 +356,7 @@
                 V((1, 128), F32),
                 V((B * BLK * 8, 64), F32), V((4, NTP, B, BLK, 128), BF16), V((4, NTP, B, BLK, 128), BF16),
                 V((4, B, D), BF16), V((4, NTP, B, D), BF16), V((B, EXP * FL), BF16), V((B, 256), BF16), V((NTP, B, 256), BF16), V((NTP, 8, 128), F32), V((NTP, 8, 128), F32), V((128, 1024), BF16),
-                DMA((11,)), DMA((4,)), DMA((2, 3)), DMA((1,)), DMA((4,)), DMA((1,)), DMA((4,)), DMA((1,)), DMA((1,)), DMA((1,)), DMA((1,)),
+                DMA((14,)), DMA((4,)), DMA((2, 3)), DMA((1,)), DMA((4,)), DMA((1,)), DMA((4,)), DMA((1,)), DMA((1,)), DMA((1,)), DMA((1,)),
             ],
             compiler_params=pltpu.CompilerParams(collective_id=0, has_side_effects=True, vmem_limit_bytes=64_000_000),
         )(hidden, lengths.reshape(1, B), jnp.transpose(choice, (0, 2, 1)), keys_one, vals_one, keys_two, vals_two,

time: 34.6 us -> 34 us (0.983)
  Pallas kernels: 33.8 us -> 33.2 us
    pallas_call x1, Pallas kernels: 32.5 us -> 31.8 us  [local_step(): pl.pallas_call(_kernel, out_shape=tuple((V(s.shape, s.dtype) for s in sha...]
where the time goes in v15:
time: 34 us; the launch traced here: 33.9 us
  Pallas kernels  33.2 us (98%)
  between operations  0.65 us (2%)
    pallas_call x1, Pallas kernels, local_step(): pl.pallas_call(_kernel, out_shape=tuple((V(s.shape, s.dtype) for s in sha...  31.8 us
    pallas_call x1, Pallas kernels, local_step(): pl.pallas_call(_store, out_shape=shapes, in_specs=[vmem_spec] * 5, out_sp...  1.36 us

profile of v15, /device:TPU:0, one launch (start us, length us, event | category | flops | bytes accessed | tf_op | source)
XLA Modules:
  0.0 33.9 jit_solution(13203185102090058491)
XLA Ops:
  0.6 31.8 %shard_map.209 = (bf16[16,1024]{1,0:T(8,128)(2,1)S(1)}, bf16[16,128,64]{2,1,0:T(8,128)(2,1)S(1)}, bf16[16,128,64]{2,1,0:T(8,128)(2,1)S(1)}, bf16[16,128,64]{2,1,0:T(8,128)(2,1)S(1)}, bf16[16,128,64]{2,1,0:T(8,128)(2,1)S(1)}) custom-call(bf16[16,1024]{1,0:T(8,128)(2,1)} %hid_h.1, s32[1,16]{1,0:T(1,128)} %bitcast.9, s32[2,8,16]{2,1,0:T(8,128)} %bitcast.8, ...), custom_call_target="tpu_custom_call" | custom-call | tf_op jit(solution)/shard_map/pallas_call | solution.py:347
  32.5 1.4 %shard_map.210 = (bf16[16,1024]{1,0:T(8,128)(2,1)}, bf16[16,128,64]{2,1,0:T(8,128)(2,1)}, bf16[16,128,64]{2,1,0:T(8,128)(2,1)}, bf16[16,128,64]{2,1,0:T(8,128)(2,1)}, bf16[16,128,64]{2,1,0:T(8,128)(2,1)}) custom-call(bf16[16,1024]{1,0:T(8,128)(2,1)S(1)} %get-tuple-element.15.h, bf16[16,128,64]{2,1,0:T(8,128)(2,1)S(1)} %get-tuple-element.16.k1, ...), custom_call_target="tpu_custom_call" | custom-call | tf_op jit(solution)/shard_map/pallas_call | solution.py:364

commit v16 on v15

--- a/solution.py
+++ b/solution.py
@@ -156,6 +156,12 @@
     for n in range(3):
         cache_send(1, n)
     raw_copy(0).wait()
+    for i in range(len(smalls)):
+        if i not in FIRST:
+            small_copy(i).wait()
+    raw_copy(2).wait()
+    raw_copy(3).wait()
+    start_layer(0)
     repack(0)
     lane8 = lax.broadcasted_iota(jnp.int32, (8, 128), 1) // BLK
     colk = lax.broadcasted_iota(jnp.int32, (64, 256), 1)
@@ -164,12 +170,6 @@
     ecol = lax.broadcasted_iota(jnp.int32, (128, 1024), 1)
     erow = lax.broadcasted_iota(jnp.int32, (128, 1024), 0)
     emat[...] = jnp.where((ecol // 256) * BLK + ecol % BLK == erow, 1.0, 0.0).astype(BF16)
-    for i in range(len(smalls)):
-        if i not in FIRST:
-            small_copy(i).wait()
-    raw_copy(2).wait()
-    raw_copy(3).wait()
-    start_layer(0)
     swapped(qx, send_q, recv_q).wait_recv()
     for p in range(NTP):
         sk = lax.dot_general(head_rows(qx[p]), snd[0, p].reshape(B * BLK, 128), (((1,), (1,)), ((), ())), preferred_element_type=F32) * 0.125

time: 34 us -> 34 us (level)
  no operation moved by 1% of the time
where the time goes in v16:
time: 34 us; the launch traced here: 33.8 us
  Pallas kernels  33.2 us (98%)
  between operations  0.65 us (2%)
    pallas_call x1, Pallas kernels, local_step(): pl.pallas_call(_kernel, out_shape=tuple((V(s.shape, s.dtype) for s in sha...  31.8 us
    pallas_call x1, Pallas kernels, local_step(): pl.pallas_call(_store, out_shape=shapes, in_specs=[vmem_spec] * 5, out_sp...  1.36 us

profile of v16, /device:TPU:0, one launch (start us, length us, event | category | flops | bytes accessed | tf_op | source)
XLA Modules:
  0.0 33.8 jit_solution(9945938148805677445)
XLA Ops:
  0.6 31.8 %shard_map.209 = (bf16[16,1024]{1,0:T(8,128)(2,1)S(1)}, bf16[16,128,64]{2,1,0:T(8,128)(2,1)S(1)}, bf16[16,128,64]{2,1,0:T(8,128)(2,1)S(1)}, bf16[16,128,64]{2,1,0:T(8,128)(2,1)S(1)}, bf16[16,128,64]{2,1,0:T(8,128)(2,1)S(1)}) custom-call(bf16[16,1024]{1,0:T(8,128)(2,1)} %hid_h.1, s32[1,16]{1,0:T(1,128)} %bitcast.9, s32[2,8,16]{2,1,0:T(8,128)} %bitcast.8, ...), custom_call_target="tpu_custom_call" | custom-call | tf_op jit(solution)/shard_map/pallas_call | solution.py:347
  32.5 1.4 %shard_map.210 = (bf16[16,1024]{1,0:T(8,128)(2,1)}, bf16[16,128,64]{2,1,0:T(8,128)(2,1)}, bf16[16,128,64]{2,1,0:T(8,128)(2,1)}, bf16[16,128,64]{2,1,0:T(8,128)(2,1)}, bf16[16,128,64]{2,1,0:T(8,128)(2,1)}) custom-call(bf16[16,1024]{1,0:T(8,128)(2,1)S(1)} %get-tuple-element.15.h, bf16[16,128,64]{2,1,0:T(8,128)(2,1)S(1)} %get-tuple-element.16.k1, ...), custom_call_target="tpu_custom_call" | custom-call | tf_op jit(solution)/shard_map/pallas_call | solution.py:364

commit v17 on v16

--- a/solution.py
+++ b/solution.py
@@ -153,8 +153,8 @@
     qx[me] = q
     raw_copy(1).wait()
     repack(1)
-    for n in range(3):
-        cache_send(1, n)
+    cache_send(1, 0)
+    cache_send(1, 2)
     raw_copy(0).wait()
     for i in range(len(smalls)):
         if i not in FIRST:
@@ -184,6 +184,7 @@
     for n in range(3):
         swap(sown.at[peers[n]], sx.at[me], send_s, recv_s, n)
     sx[me] = sown[me]
+    cache_send(1, 1)
     repack(2)
     cache_send(2, 0)
     cache_send(2, 2)

time: 34 us -> 34 us (level)
  no operation moved by 1% of the time
where the time goes in v17:
time: 34 us; the launch traced here: 33.9 us
  Pallas kernels  33.2 us (98%)
  between operations  0.65 us (2%)
    pallas_call x1, Pallas kernels, local_step(): pl.pallas_call(_kernel, out_shape=tuple((V(s.shape, s.dtype) for s in sha...  31.9 us
    pallas_call x1, Pallas kernels, local_step(): pl.pallas_call(_store, out_shape=shapes, in_specs=[vmem_spec] * 5, out_sp...  1.36 us

profile of v17, /device:TPU:0, one launch (start us, length us, event | category | flops | bytes accessed | tf_op | source)
XLA Modules:
  0.0 33.9 jit_solution(18043486254756903189)
XLA Ops:
  0.6 31.9 %shard_map.209 = (bf16[16,1024]{1,0:T(8,128)(2,1)S(1)}, bf16[16,128,64]{2,1,0:T(8,128)(2,1)S(1)}, bf16[16,128,64]{2,1,0:T(8,128)(2,1)S(1)}, bf16[16,128,64]{2,1,0:T(8,128)(2,1)S(1)}, bf16[16,128,64]{2,1,0:T(8,128)(2,1)S(1)}) custom-call(bf16[16,1024]{1,0:T(8,128)(2,1)} %hid_h.1, s32[1,16]{1,0:T(1,128)} %bitcast.9, s32[2,8,16]{2,1,0:T(8,128)} %bitcast.8, ...), custom_call_target="tpu_custom_call" | custom-call | tf_op jit(solution)/shard_map/pallas_call | solution.py:348
  32.5 1.4 %shard_map.210 = (bf16[16,1024]{1,0:T(8,128)(2,1)}, bf16[16,128,64]{2,1,0:T(8,128)(2,1)}, bf16[16,128,64]{2,1,0:T(8,128)(2,1)}, bf16[16,128,64]{2,1,0:T(8,128)(2,1)}, bf16[16,128,64]{2,1,0:T(8,128)(2,1)}) custom-call(bf16[16,1024]{1,0:T(8,128)(2,1)S(1)} %get-tuple-element.15.h, bf16[16,128,64]{2,1,0:T(8,128)(2,1)S(1)} %get-tuple-element.16.k1, ...), custom_call_target="tpu_custom_call" | custom-call | tf_op jit(solution)/shard_map/pallas_call | solution.py:365
